TPU v7x, 32 devices: a whole 2x2x4 slice. The times are simulated.
32 devices in a mesh: gx: 8 (over z, core), gy: 2 (over y), gz: 2 (over x).
Axes of the slice: x: 2, y: 2, z: 4, core: 2. Of those that a mesh axis runs over, the one named last changes fastest.
Arguments:
- volume: float32 [128, 128, 256], P('gx', 'gy', 'gz'), may hold values from -6 to 6
- weights: float32 [64, 8, 128], P(None, None, 'gx'), may hold values from -0.1875 to 0.1875
- offsets: int32 [64, 8], P(None, 'gx'), may hold values from 0 to 57, as said below
- measured: float32 [64, 128, 256], P('gx', 'gy', 'gz'), may hold values from -6 to 6
Outputs:
- gradient: float32 [128, 128, 256], P('gx', 'gy', 'gz')
- residual: float32 [64, 128, 256], P('gx', 'gy', 'gz')
- misfit: float32 [], replicated
Inputs may be any that keep to these rules, and one draw needn't show every extreme that they name: offsets[a, b] shifts angle a on brick b; the values 0 and 57 both occur.
All inputs are finite; a program needn't handle non-finite values.
Results may differ from a plain program's by a relative error of at most 0.0003.
Values sent between devices are 32-bit elements; how exact they have to be, the bound alone decides.
No kernel may reach another device: no remote copies, remote signals or barrier semaphores. Data moves between devices by JAX's collectives and lax.ppermute only.
A program may use at most 64 MiB of HBM per device.

v0:
```python
import jax
import jax.numpy as jnp
from jax import lax
from jax.sharding import PartitionSpec as P


def passed_along(x, axis, by):
    count = lax.axis_size(axis)
    pairs = [(i, i + by) for i in range(count) if 0 <= i + by < count]
    return lax.ppermute(x, axis, pairs)


def body(volume, weights, offsets, measured):
    cols, rows, depth = volume.shape
    angles = weights.shape[0]
    taps = weights.shape[1]
    blocks = angles // 8
    shifts = offsets[:, 0]
    wblk = weights.reshape(blocks, 8, taps, cols)
    sblk = shifts.reshape(blocks, 8)

    def project(args):
        wb, sb = args
        spread = jnp.einsum("adc,cyz->adyz", wb, volume, precision=lax.Precision.HIGHEST)
        padded = jnp.pad(spread, ((0, 0), (0, 0), (rows, rows), (0, 0)))

        def project_per_angle(plane, shift):
            window = lax.dynamic_slice_in_dim(plane, shift, 2 * rows + taps - 1, 1)
            total = jnp.zeros((2 * rows, depth), jnp.float32)
            for tap in range(taps):
                total = total + window[tap, tap : tap + 2 * rows]
            return total

        return jax.vmap(project_per_angle)(padded, sb)

    window_rows = lax.map(project, (wblk, sblk)).reshape(angles, 2 * rows, depth)
    lower = window_rows[:, :rows]
    upper = window_rows[:, rows:]
    partial_value = upper + passed_along(lower, "gy", -1)
    summed = lax.psum_scatter(partial_value, "gx", scatter_dimension=0, tiled=True)
    resid_share = summed - measured
    before = passed_along(resid_share, "gy", 1)
    resid_all, before_all = (
        lax.all_gather(resid_share, "gx", axis=0, tiled=True),
        lax.all_gather(before, "gx", axis=0, tiled=True),
    )
    extended = jnp.concatenate([before_all, resid_all], axis=1)
    rblk = extended.reshape(blocks, 8, 2 * rows, depth)

    def backward(grad, args):
        wb, sb, rb = args

        def backward_per_angle(plane, shift):
            start = rows - shift - (taps - 1)
            window = lax.dynamic_slice_in_dim(plane, start, rows + taps - 1, 0)
            return jnp.stack(
                [window[taps - 1 - tap : taps - 1 - tap + rows] for tap in range(taps)]
            )

        sheared = jax.vmap(backward_per_angle)(rb, sb)
        grad = grad + jnp.einsum("adc,adyz->cyz", wb, sheared, precision=lax.Precision.HIGHEST)
        return (grad, None)

    gradient, unused = lax.scan(
        backward, jnp.zeros((cols, rows, depth), jnp.float32), (wblk, sblk, rblk)
    )
    entries = angles * rows * depth * lax.axis_size("gy") * lax.axis_size("gz")
    misfit = lax.psum(jnp.sum(resid_share * resid_share), ("gx", "gy", "gz")) / entries
    return (gradient, resid_share, misfit)


def solution(mesh):
    in_specs = (P("gx", "gy", "gz"), P(None, None, "gx"), P(None, "gx"), P("gx", "gy", "gz"))
    out_specs = (P("gx", "gy", "gz"), P("gx", "gy", "gz"), P())
    return jax.shard_map(body, mesh=mesh, in_specs=in_specs, out_specs=out_specs, check_vma=False)
```

profile of v0, /device:TPU:0, one launch (start us, length us, event | category | flops | bytes accessed | tf_op | source)
XLA Modules:
  0.0 486.3 jit_solution(15363461617519916820)
XLA Ops:
  12.2 215.0 %while.27 = (s32[]{:T(128)}, f32[8,8,128,128]{3,2,1,0:T(8,128)}, f32[8,8,8,16]{3,2,1,0:T(8,128)}, f32[16,64,128]{2,0,1:T(8,128)S(1)}, s32[8,8]{1,0:T(8,128)S(1)}, /*index=5*/s32[]{:T(128)}, f32[]{:T(128)}) while((s32[]{:T(128)}, f32[8,8,128,128]{3,2,1,0:T(8,128)}, f32[8,8,8,16]{3,2,1,0:T(8,128)}, f32[16,64,128]{2,0,1:T(8,128)S(1)}, ...), condition=%wide.region_1.2_spmd, body=%wide.region_0.1_spmd.sunk | while | flops 101580864 | bytes 29852948 | solution.py:36
  18.5 6.1 %gather_fusion = f32[8,8,135,128]{3,1,2,0:T(8,128)} fusion(f32[8,8,192,128]{3,1,0,2:T(8,128)} %pad.13.clone.2, s32[8]{0:T(128)S(1)} %or_bitcast_fusion.4), kind=kCustom, calls=%fused_computation.clone.1 | custom fusion | bytes 8847488 | tf_op jit(solution)/shard_map/while/body/eval_jaxpr/vmap()/gather | solution.py:28
  24.6 13.6 %slice_add_fusion.9 = f32[8,1,128,128]{3,1,2,0:T(1,128)S(1)} fusion(f32[8,8,135,128]{3,1,2,0:T(8,128)} %gather_fusion), kind=kLoop, calls=%fused_computation.2.clone.1 | loop fusion | flops 917504 | bytes 4718592 | tf_op jit(solution)/shard_map/while/body/eval_jaxpr/vmap()/add | solution.py:31
  45.4 6.1 %gather_fusion = f32[8,8,135,128]{3,1,2,0:T(8,128)} fusion(f32[8,8,192,128]{3,1,0,2:T(8,128)} %pad.13.clone.2, s32[8]{0:T(128)S(1)} %or_bitcast_fusion.4), kind=kCustom, calls=%fused_computation.clone.1 | custom fusion | bytes 8847488 | tf_op jit(solution)/shard_map/while/body/eval_jaxpr/vmap()/gather | solution.py:28
  51.5 13.6 %slice_add_fusion.9 = f32[8,1,128,128]{3,1,2,0:T(1,128)S(1)} fusion(f32[8,8,135,128]{3,1,2,0:T(8,128)} %gather_fusion), kind=kLoop, calls=%fused_computation.2.clone.1 | loop fusion | flops 917504 | bytes 4718592 | tf_op jit(solution)/shard_map/while/body/eval_jaxpr/vmap()/add | solution.py:31
  72.3 6.1 %gather_fusion = f32[8,8,135,128]{3,1,2,0:T(8,128)} fusion(f32[8,8,192,128]{3,1,0,2:T(8,128)} %pad.13.clone.2, s32[8]{0:T(128)S(1)} %or_bitcast_fusion.4), kind=kCustom, calls=%fused_computation.clone.1 | custom fusion | bytes 8847488 | tf_op jit(solution)/shard_map/while/body/eval_jaxpr/vmap()/gather | solution.py:28
  78.3 13.6 %slice_add_fusion.9 = f32[8,1,128,128]{3,1,2,0:T(1,128)S(1)} fusion(f32[8,8,135,128]{3,1,2,0:T(8,128)} %gather_fusion), kind=kLoop, calls=%fused_computation.2.clone.1 | loop fusion | flops 917504 | bytes 4718592 | tf_op jit(solution)/shard_map/while/body/eval_jaxpr/vmap()/add | solution.py:31
  99.1 6.1 %gather_fusion = f32[8,8,135,128]{3,1,2,0:T(8,128)} fusion(f32[8,8,192,128]{3,1,0,2:T(8,128)} %pad.13.clone.2, s32[8]{0:T(128)S(1)} %or_bitcast_fusion.4), kind=kCustom, calls=%fused_computation.clone.1 | custom fusion | bytes 8847488 | tf_op jit(solution)/shard_map/while/body/eval_jaxpr/vmap()/gather | solution.py:28
  105.2 13.6 %slice_add_fusion.9 = f32[8,1,128,128]{3,1,2,0:T(1,128)S(1)} fusion(f32[8,8,135,128]{3,1,2,0:T(8,128)} %gather_fusion), kind=kLoop, calls=%fused_computation.2.clone.1 | loop fusion | flops 917504 | bytes 4718592 | tf_op jit(solution)/shard_map/while/body/eval_jaxpr/vmap()/add | solution.py:31
  126.0 6.1 %gather_fusion = f32[8,8,135,128]{3,1,2,0:T(8,128)} fusion(f32[8,8,192,128]{3,1,0,2:T(8,128)} %pad.13.clone.2, s32[8]{0:T(128)S(1)} %or_bitcast_fusion.4), kind=kCustom, calls=%fused_computation.clone.1 | custom fusion | bytes 8847488 | tf_op jit(solution)/shard_map/while/body/eval_jaxpr/vmap()/gather | solution.py:28
  132.1 13.6 %slice_add_fusion.9 = f32[8,1,128,128]{3,1,2,0:T(1,128)S(1)} fusion(f32[8,8,135,128]{3,1,2,0:T(8,128)} %gather_fusion), kind=kLoop, calls=%fused_computation.2.clone.1 | loop fusion | flops 917504 | bytes 4718592 | tf_op jit(solution)/shard_map/while/body/eval_jaxpr/vmap()/add | solution.py:31
  152.9 6.1 %gather_fusion = f32[8,8,135,128]{3,1,2,0:T(8,128)} fusion(f32[8,8,192,128]{3,1,0,2:T(8,128)} %pad.13.clone.2, s32[8]{0:T(128)S(1)} %or_bitcast_fusion.4), kind=kCustom, calls=%fused_computation.clone.1 | custom fusion | bytes 8847488 | tf_op jit(solution)/shard_map/while/body/eval_jaxpr/vmap()/gather | solution.py:28
  159.0 13.6 %slice_add_fusion.9 = f32[8,1,128,128]{3,1,2,0:T(1,128)S(1)} fusion(f32[8,8,135,128]{3,1,2,0:T(8,128)} %gather_fusion), kind=kLoop, calls=%fused_computation.2.clone.1 | loop fusion | flops 917504 | bytes 4718592 | tf_op jit(solution)/shard_map/while/body/eval_jaxpr/vmap()/add | solution.py:31
  179.8 6.1 %gather_fusion = f32[8,8,135,128]{3,1,2,0:T(8,128)} fusion(f32[8,8,192,128]{3,1,0,2:T(8,128)} %pad.13.clone.2, s32[8]{0:T(128)S(1)} %or_bitcast_fusion.4), kind=kCustom, calls=%fused_computation.clone.1 | custom fusion | bytes 8847488 | tf_op jit(solution)/shard_map/while/body/eval_jaxpr/vmap()/gather | solution.py:28
  185.9 13.6 %slice_add_fusion.9 = f32[8,1,128,128]{3,1,2,0:T(1,128)S(1)} fusion(f32[8,8,135,128]{3,1,2,0:T(8,128)} %gather_fusion), kind=kLoop, calls=%fused_computation.2.clone.1 | loop fusion | flops 917504 | bytes 4718592 | tf_op jit(solution)/shard_map/while/body/eval_jaxpr/vmap()/add | solution.py:31
  206.7 6.1 %gather_fusion = f32[8,8,135,128]{3,1,2,0:T(8,128)} fusion(f32[8,8,192,128]{3,1,0,2:T(8,128)} %pad.13.clone.2, s32[8]{0:T(128)S(1)} %or_bitcast_fusion.4), kind=kCustom, calls=%fused_computation.clone.1 | custom fusion | bytes 8847488 | tf_op jit(solution)/shard_map/while/body/eval_jaxpr/vmap()/gather | solution.py:28
  212.8 13.6 %slice_add_fusion.9 = f32[8,1,128,128]{3,1,2,0:T(1,128)S(1)} fusion(f32[8,8,135,128]{3,1,2,0:T(8,128)} %gather_fusion), kind=kLoop, calls=%fused_computation.2.clone.1 | loop fusion | flops 917504 | bytes 4718592 | tf_op jit(solution)/shard_map/while/body/eval_jaxpr/vmap()/add | solution.py:31
  230.4 48.6 %collective-permute-done = f32[64,64,128]{2,1,0:T(8,128)S(1)} collective-permute-done((f32[64,64,128]{2,1,0:T(8,128)S(1)}, f32[64,64,128]{2,1,0:T(8,128)S(1)}, u32[]{:S(2)}, u32[]{:S(2)}) %collective-permute-start) | collective-permute-done | bytes 2097184 | tf_op jit(solution)/shard_map/ppermute | solution.py:10
  282.4 37.3 %reduce-scatter.2.cloned.1.call-done = f32[8,64,128]{2,1,0:T(8,128)} async-done(((f32[64,64,128]{2,1,0:T(8,128)}), f32[8,64,128]{2,1,0:T(8,128)}) %reduce-scatter.2.cloned.1.call-update) | async-done | bytes 262160 | tf_op jit(solution)/shard_map/reduce_scatter | solution.py:40
  325.4 4.2 collective-permute-done.1
  330.3 39.0 %psum.7 = f32[]{:T(128)} all-reduce(f32[]{:T(128)} %get-tuple-element.237), channel_id=1, replica_groups=mesh['gx'=8,'gy'=2,'gz'=2] {'gx','gy','gz'}, use_global_device_ids=true, to_apply=%region_6.7 | all-reduce | flops 1 | bytes 8 | tf_op jit(solution)/shard_map/psum | solution.py:68
  370.0 10.4 %all-gather.3.cloned.1.call-done = f32[64,64,128]{2,1,0:T(8,128)} async-done(((f32[8,64,128]{2,1,0:T(8,128)}), f32[64,64,128]{2,1,0:T(8,128)}) %all-gather.3.cloned.1.call-update) | async-done | bytes 2097168 | tf_op jit(solution)/shard_map/all_gather | solution.py:45
  380.4 4.7 pad_maximum_fusion
  385.1 91.6 %while.28 = (s32[]{:T(128)}, f32[16,64,128]{2,0,1:T(8,128)}, f32[8,8,8,16]{3,2,1,0:T(8,128)}, f32[8,8,128,128]{3,2,1,0:T(8,128)}, s32[8,8]{1,0:T(8,128)S(1)}, /*index=5*/s32[]{:T(128)}, s32[]{:T(128)}) while((s32[]{:T(128)}, f32[16,64,128]{2,0,1:T(8,128)}, f32[8,8,8,16]{3,2,1,0:T(8,128)}, f32[8,8,128,128]{3,2,1,0:T(8,128)}, ...), condition=%wide.region_4.5_spmd.clone, body=%wide.region_3.4_spmd.clone.sunk | while | flops 100925512 | bytes 14246655 | solution.py:64
  388.4 5.1 %stack.91 = f32[8,8,64,128]{3,0,1,2:T(8,128)S(1)} concatenate(f32[1,8,64,128]{3,0,1,2:T(1,128)} %bitcast.108, f32[1,8,64,128]{3,0,1,2:T(1,128)} %bitcast.107, f32[1,8,64,128]{3,0,1,2:T(1,128)} %bitcast.106, f32[1,8,64,128]{3,0,1,2:T(1,128)S(1)} %bitcast.105, f32[1,8,64,128]{3,0,1,2:T(1,128)S(1)} %bitcast.104, f32[1,8,64,128]{3,0,1,2:T(1,128)S(1)} %bitcast.103, ...), dimensions={0} | concatenate | bytes 4194304 | tf_op jit(solution)/shard_map/while/body/eval_jaxpr/vmap()/stack | solution.py:56
  399.6 5.1 %stack.91 = f32[8,8,64,128]{3,0,1,2:T(8,128)S(1)} concatenate(f32[1,8,64,128]{3,0,1,2:T(1,128)} %bitcast.108, f32[1,8,64,128]{3,0,1,2:T(1,128)} %bitcast.107, f32[1,8,64,128]{3,0,1,2:T(1,128)} %bitcast.106, f32[1,8,64,128]{3,0,1,2:T(1,128)S(1)} %bitcast.105, f32[1,8,64,128]{3,0,1,2:T(1,128)S(1)} %bitcast.104, f32[1,8,64,128]{3,0,1,2:T(1,128)S(1)} %bitcast.103, ...), dimensions={0} | concatenate | bytes 4194304 | tf_op jit(solution)/shard_map/while/body/eval_jaxpr/vmap()/stack | solution.py:56
  411.1 5.1 %stack.91 = f32[8,8,64,128]{3,0,1,2:T(8,128)S(1)} concatenate(f32[1,8,64,128]{3,0,1,2:T(1,128)} %bitcast.108, f32[1,8,64,128]{3,0,1,2:T(1,128)} %bitcast.107, f32[1,8,64,128]{3,0,1,2:T(1,128)} %bitcast.106, f32[1,8,64,128]{3,0,1,2:T(1,128)S(1)} %bitcast.105, f32[1,8,64,128]{3,0,1,2:T(1,128)S(1)} %bitcast.104, f32[1,8,64,128]{3,0,1,2:T(1,128)S(1)} %bitcast.103, ...), dimensions={0} | concatenate | bytes 4194304 | tf_op jit(solution)/shard_map/while/body/eval_jaxpr/vmap()/stack | solution.py:56
  422.6 5.1 %stack.91 = f32[8,8,64,128]{3,0,1,2:T(8,128)S(1)} concatenate(f32[1,8,64,128]{3,0,1,2:T(1,128)} %bitcast.108, f32[1,8,64,128]{3,0,1,2:T(1,128)} %bitcast.107, f32[1,8,64,128]{3,0,1,2:T(1,128)} %bitcast.106, f32[1,8,64,128]{3,0,1,2:T(1,128)S(1)} %bitcast.105, f32[1,8,64,128]{3,0,1,2:T(1,128)S(1)} %bitcast.104, f32[1,8,64,128]{3,0,1,2:T(1,128)S(1)} %bitcast.103, ...), dimensions={0} | concatenate | bytes 4194304 | tf_op jit(solution)/shard_map/while/body/eval_jaxpr/vmap()/stack | solution.py:56
  434.1 5.1 %stack.91 = f32[8,8,64,128]{3,0,1,2:T(8,128)S(1)} concatenate(f32[1,8,64,128]{3,0,1,2:T(1,128)} %bitcast.108, f32[1,8,64,128]{3,0,1,2:T(1,128)} %bitcast.107, f32[1,8,64,128]{3,0,1,2:T(1,128)} %bitcast.106, f32[1,8,64,128]{3,0,1,2:T(1,128)S(1)} %bitcast.105, f32[1,8,64,128]{3,0,1,2:T(1,128)S(1)} %bitcast.104, f32[1,8,64,128]{3,0,1,2:T(1,128)S(1)} %bitcast.103, ...), dimensions={0} | concatenate | bytes 4194304 | tf_op jit(solution)/shard_map/while/body/eval_jaxpr/vmap()/stack | solution.py:56
  445.5 5.1 %stack.91 = f32[8,8,64,128]{3,0,1,2:T(8,128)S(1)} concatenate(f32[1,8,64,128]{3,0,1,2:T(1,128)} %bitcast.108, f32[1,8,64,128]{3,0,1,2:T(1,128)} %bitcast.107, f32[1,8,64,128]{3,0,1,2:T(1,128)} %bitcast.106, f32[1,8,64,128]{3,0,1,2:T(1,128)S(1)} %bitcast.105, f32[1,8,64,128]{3,0,1,2:T(1,128)S(1)} %bitcast.104, f32[1,8,64,128]{3,0,1,2:T(1,128)S(1)} %bitcast.103, ...), dimensions={0} | concatenate | bytes 4194304 | tf_op jit(solution)/shard_map/while/body/eval_jaxpr/vmap()/stack | solution.py:56
  457.0 5.1 %stack.91 = f32[8,8,64,128]{3,0,1,2:T(8,128)S(1)} concatenate(f32[1,8,64,128]{3,0,1,2:T(1,128)} %bitcast.108, f32[1,8,64,128]{3,0,1,2:T(1,128)} %bitcast.107, f32[1,8,64,128]{3,0,1,2:T(1,128)} %bitcast.106, f32[1,8,64,128]{3,0,1,2:T(1,128)S(1)} %bitcast.105, f32[1,8,64,128]{3,0,1,2:T(1,128)S(1)} %bitcast.104, f32[1,8,64,128]{3,0,1,2:T(1,128)S(1)} %bitcast.103, ...), dimensions={0} | concatenate | bytes 4194304 | tf_op jit(solution)/shard_map/while/body/eval_jaxpr/vmap()/stack | solution.py:56
  468.5 5.1 %stack.91 = f32[8,8,64,128]{3,0,1,2:T(8,128)S(1)} concatenate(f32[1,8,64,128]{3,0,1,2:T(1,128)} %bitcast.108, f32[1,8,64,128]{3,0,1,2:T(1,128)} %bitcast.107, f32[1,8,64,128]{3,0,1,2:T(1,128)} %bitcast.106, f32[1,8,64,128]{3,0,1,2:T(1,128)S(1)} %bitcast.105, f32[1,8,64,128]{3,0,1,2:T(1,128)S(1)} %bitcast.104, f32[1,8,64,128]{3,0,1,2:T(1,128)S(1)} %bitcast.103, ...), dimensions={0} | concatenate | bytes 4194304 | tf_op jit(solution)/shard_map/while/body/eval_jaxpr/vmap()/stack | solution.py:56
  (112 shorter events, 128.2 us)
Async XLA Ops:
  7.2 312.5 %reduce-scatter.2.cloned.1.call-start = ((), (), s32[]{:S(2)}) async-start(), calls=%async_computation.1 | async-start | bytes 2359296 | tf_op jit(solution)/shard_map/reduce_scatter | solution.py:40
  228.9 90.7 %copy-start.1 = (f32[8,64,128]{2,1,0:T(8,128)S(1)}, f32[8,64,128]{2,1,0:T(8,128)}, u32[]{:S(2)}) copy-start(f32[8,64,128]{2,1,0:T(8,128)} %param.11) | copy-start | bytes 786436
  228.9 50.1 %collective-permute-start = (f32[64,64,128]{2,1,0:T(8,128)S(1)}, f32[64,64,128]{2,1,0:T(8,128)S(1)}, u32[]{:S(2)}, u32[]{:S(2)}) collective-permute-start(f32[64,64,128]{2,1,0:T(8,128)S(1)} %slice.162), channel_id=1, source_target_pairs={{2,0},{3,1},{6,4},{7,5},{10,8},{11,9},{14,12},{15,13},{18,16},{19,... | collective-permute-start | bytes 6291464 | tf_op jit(solution)/shard_map/ppermute | solution.py:10
  282.4 87.6 %all-gather.5.cloned.1.call-start = ((), (), s32[]{:S(2)}) async-start(), calls=%async_computation.3 | async-start | bytes 2359296 | tf_op jit(solution)/shard_map/all_gather | solution.py:44
  322.0 58.4 %all-gather.3.cloned.1.call-start = ((), (), s32[]{:S(2)}) async-start(), calls=%async_computation.2 | async-start | bytes 2359296 | tf_op jit(solution)/shard_map/all_gather | solution.py:45
  322.0 7.6 %collective-permute-start.1 = (f32[8,64,128]{2,1,0:T(8,128)}, f32[8,64,128]{2,1,0:T(8,128)S(1)}, u32[]{:S(2)}, u32[]{:S(2)}) collective-permute-start(f32[8,64,128]{2,1,0:T(8,128)} %get-tuple-element.238), channel_id=1, source_target_pairs={{0,2},{1,3},{4,6},{5,7},{8,10},{9,11},{12,14},{13,15},{16,18},{17,... | collective-permute-start | bytes 786440 | tf_op jit(solution)/shard_map/ppermute | solution.py:10
  329.6 0.7 copy-start
Sparse Core Ops, SparseCore 0:
  282.5 37.1 reduce-scatter.1
  322.1 27.9 all-gather.4
  351.7 28.7 all-gather.2
where the time goes:
time: 491 us; the launch traced here: 486 us
  local copies, waits for them, and re-layouts  161 us (33%)
  other arithmetic  120 us (24%)
  waiting for transfers between devices  101 us (21%)
  matrix products  44 us (9%)
  blocking collectives  39 us (8%)
  between operations  15.6 us (3%)
  starting transfers between devices  4.94 us (1%)
    add x8, other arithmetic, project_per_angle(): total = total + window[tap, tap:tap + 2 * rows]  109 us
    ppermute x2, waiting for transfers between devices, passed_along(): return lax.ppermute(x, axis, pairs)  52.8 us
    gather x8, local copies, waits for them, and re-layouts, project_per_angle(): window = lax.dynamic_slice_in_dim(plane, shift, 2 * rows + taps - 1, 1)  48.6 us
    another operation x8, local copies, waits for them, and re-layouts, backward_per_angle(): jnp.stack([window[taps - 1 - tap:taps - 1 - tap + rows] for tap in range(...  40.8 us
    psum x1, blocking collectives, body(): lax.psum(jnp.sum(resid_share * resid_share), ('gx', 'gy', 'gz')) / entries  39 us
    reduce_scatter x1, waiting for transfers between devices, body(): lax.psum_scatter(partial_value, 'gx', scatter_dimension=0, tiled=True)  37.3 us
    pad x8, local copies, waits for them, and re-layouts, project(): padded = jnp.pad(spread, ((0, 0), (0, 0), (rows, rows), (0, 0)))  28.4 us
    dot_general x8, matrix products, backward(): jnp.einsum('adc,adyz->cyz', wb, sheared, precision=lax.Precision.HIGHEST)  23.8 us
  transfers between devices with their start and end apart: 5, of which 4 were waited for; matrix products, arithmetic and copies ran while one was open for 0% of the time, Pallas kernels for 0%

commit v1 on v0

--- a/solution.py
+++ b/solution.py
@@ -1,7 +1,170 @@
+import functools
+
 import jax
 import jax.numpy as jnp
 from jax import lax
+from jax.experimental import pallas as pl
+from jax.experimental.pallas import tpu as pltpu
 from jax.sharding import PartitionSpec as P
+
+LANES = 128
+SUBS = 8
+
+
+def split(x):
+    high = x.astype(jnp.bfloat16)
+    low = (x - high.astype(jnp.float32)).astype(jnp.bfloat16)
+    return high, low
+
+
+def lane_ids(rows):
+    return lax.broadcasted_iota(jnp.int32, (rows, LANES), 1)
+
+
+def swap(x):
+    return pltpu.roll(x, LANES // 2, 1)
+
+
+def unpair(first, second):
+    left = lane_ids(first.shape[0]) < LANES // 2
+    return jnp.where(left, first, swap(second)), jnp.where(left, swap(first), second)
+
+
+def pack_kernel(half_rows, vol_ref, meas_ref, w_ref, off_ref, out_ref, flat_ref):
+    cols, rows, depth = vol_ref.shape
+    share = meas_ref.shape[0]
+    angles, taps, _ = w_ref.shape
+    peers = out_ref.shape[0]
+    deep = depth // peers
+    at = 0
+    for ref, count in ((vol_ref, cols // 2), (meas_ref, share // 2)):
+        for j in range(count):
+            pair = jnp.concatenate([ref[j], ref[j + count]], axis=0)
+            out_ref[:, at : at + deep, :] = pair.T.reshape(peers, deep, LANES)
+            at += deep
+    for tap in range(taps):
+        flat_ref[:, tap * cols : (tap + 1) * cols] = w_ref[:, tap, :]
+    start = pl.multiple_of(lax.axis_index("gy") * half_rows, SUBS)
+    part = flat_ref[pl.ds(start, half_rows), :]
+    out_ref[:, at : at + half_rows, :] = jnp.broadcast_to(part, (peers, half_rows, LANES))
+    at += half_rows
+    shift = jnp.broadcast_to(off_ref[...].astype(jnp.float32), (angles, LANES))
+    shift = jnp.concatenate([shift, jnp.zeros((LANES - angles, LANES), jnp.float32)], axis=0)
+    out_ref[:, at : at + SUBS, :] = jnp.broadcast_to(shift.T[:SUBS], (peers, SUBS, LANES))
+
+
+def main_kernel(dims, in_ref, out_ref, wf_ref, wb_ref, sh_ref, sq_ref):
+    bricks, groups, cols, taps, angles, share, deep = dims
+    wide = taps * cols
+    piece = angles // groups
+    w_at = (cols // 2 + share // 2) * deep
+    s_at = w_at + piece
+    m_at = (cols // 2) * deep
+    quarter = share // 2
+    for i in range(bricks):
+        w = jnp.concatenate([in_ref[i * groups + h, w_at : w_at + piece, :] for h in range(groups)], axis=0)
+        high, low = split(w)
+        wf_ref[i, :angles, :wide] = high
+        wf_ref[i, :angles, wide:] = high
+        wf_ref[i, angles:, :wide] = low
+        wf_ref[i, angles:, wide:] = jnp.zeros_like(low)
+        high, low = split(w.T)
+        wb_ref[i, :wide, :angles] = high
+        wb_ref[i, :wide, angles:] = high
+        wb_ref[i, wide:, :angles] = low
+        wb_ref[i, wide:, angles:] = jnp.zeros_like(low)
+        row = in_ref[i * groups, s_at : s_at + SUBS, :]
+        sh_ref[i] = jnp.concatenate([row] * (LANES // SUBS), axis=0).T[:angles].astype(jnp.int32)
+    sq_ref[...] = jnp.zeros_like(sq_ref)
+    lane_a = lane_ids(angles)
+    lane_c = lane_ids(cols)
+
+    def pair_of_depths(q, carry):
+        zs = [2 * q, 2 * q + 1]
+        accs = [jnp.zeros((angles, LANES), jnp.float32) for _ in zs]
+        for i in range(bricks):
+            blocks = []
+            for z in zs:
+                first, second = (in_ref[i * groups + h, pl.ds(z, cols // 2, stride=deep), :] for h in range(2))
+                x = jnp.concatenate(unpair(first, second), axis=0)
+                moved = [x]
+                for tap in range(1, taps):
+                    moved.append(jnp.where(lane_c < LANES - tap, pltpu.roll(x, LANES - tap, 1), 0.0))
+                blocks.append(jnp.concatenate(split(jnp.concatenate(moved, axis=0)), axis=0))
+            out = jnp.dot(wf_ref[i], jnp.concatenate(blocks, axis=1), preferred_element_type=jnp.float32)
+            out = out[:angles] + out[angles:]
+            reach = lane_a + sh_ref[i]
+            index = reach & (LANES - 1)
+            for k in range(2):
+                part = out[:, k * LANES : (k + 1) * LANES]
+                part = jnp.take_along_axis(part, index, axis=1, mode="promise_in_bounds")
+                accs[k] = accs[k] + jnp.where(reach < LANES, part, 0.0)
+        resids = []
+        for k, z in enumerate(zs):
+            rows = []
+            for i in range(bricks):
+                first, second = (in_ref[i * groups + h, pl.ds(m_at + z, quarter, stride=deep), :] for h in range(2))
+                rows.extend(unpair(first, second))
+            resid = accs[k] - jnp.concatenate(rows, axis=0)
+            square = resid * resid
+            for at in range(0, angles, SUBS):
+                sq_ref[...] += square[at : at + SUBS]
+            resids.append(resid)
+            for i in range(bricks):
+                low = resid[i * share : i * share + quarter]
+                high = resid[i * share + quarter : (i + 1) * share]
+                for h, block in enumerate(unpair(low, high)):
+                    out_ref[i * groups + h, pl.ds(m_at + z, quarter, stride=deep), :] = block
+        for i in range(bricks):
+            back = lane_a - sh_ref[i]
+            index = back & (LANES - 1)
+            blocks = []
+            for k in range(2):
+                part = jnp.take_along_axis(resids[k], index, axis=1, mode="promise_in_bounds")
+                part = jnp.where(back >= 0, part, 0.0)
+                blocks.append(jnp.concatenate(split(part), axis=0))
+            out = jnp.dot(wb_ref[i], jnp.concatenate(blocks, axis=1), preferred_element_type=jnp.float32)
+            out = out[:wide] + out[wide:]
+            for k, z in enumerate(zs):
+                part = out[:, k * LANES : (k + 1) * LANES]
+                total = part[:cols]
+                for tap in range(1, taps):
+                    total = total + jnp.where(lane_c >= tap, pltpu.roll(part[tap * cols : (tap + 1) * cols], tap, 1), 0.0)
+                for h, block in enumerate(unpair(total[: cols // 2], total[cols // 2 :])):
+                    out_ref[i * groups + h, pl.ds(z, cols // 2, stride=deep), :] = block
+        return carry
+
+    lax.fori_loop(0, deep // 2, pair_of_depths, 0)
+    m_end = m_at + quarter * deep
+    for p in range(bricks * groups):
+        out_ref[p, m_end : m_end + SUBS, :] = sq_ref[...]
+
+
+def unpack_kernel(in_ref, grad_ref, res_ref, sq_ref):
+    peers = in_ref.shape[0]
+    cols, rows, depth = grad_ref.shape
+    share = res_ref.shape[0]
+    deep = depth // peers
+    at = 0
+    for ref, count in ((grad_ref, cols // 2), (res_ref, share // 2)):
+        for j in range(count):
+            both = in_ref[:, at : at + deep, :].reshape(depth, LANES).T
+            ref[j] = both[:rows]
+            ref[j + count] = both[rows:]
+            at += deep
+    total = in_ref[0, at : at + SUBS, :]
+    for p in range(1, peers):
+        total = total + in_ref[p, at : at + SUBS, :]
+    sq_ref[...] = total
+
+
+def butterfly(x, axis):
+    count = lax.axis_size(axis)
+    step = 1
+    while step < count:
+        x = x + lax.ppermute(x, axis, [(i, i ^ step) for i in range(count)])
+        step *= 2
+    return x
 
 
 def passed_along(x, axis, by):
@@ -10,7 +173,7 @@
     return lax.ppermute(x, axis, pairs)
 
 
-def body(volume, weights, offsets, measured):
+def general(volume, weights, offsets, measured):
     cols, rows, depth = volume.shape
     angles = weights.shape[0]
     taps = weights.shape[1]
@@ -69,6 +232,73 @@
     return (gradient, resid_share, misfit)
 
 
+def fits(volume, weights, measured):
+    cols, rows, depth = volume.shape
+    angles, taps, _ = weights.shape
+    groups = lax.axis_size("gy")
+    deep, rest = divmod(depth, lax.axis_size("gx") * groups)
+    return (
+        groups == 2
+        and 2 * rows == LANES
+        and depth == LANES
+        and rest == 0
+        and deep == SUBS
+        and cols == 2 * SUBS
+        and taps * cols == LANES
+        and angles == LANES // 2
+        and measured.shape[0] == SUBS
+    )
+
+
+def body(volume, weights, offsets, measured):
+    cols, rows, depth = volume.shape
+    angles, taps, _ = weights.shape
+    if not fits(volume, weights, measured):
+        return general(volume, weights, offsets, measured)
+    share = measured.shape[0]
+    bricks = lax.axis_size("gx")
+    groups = lax.axis_size("gy")
+    peers = bricks * groups
+    deep = depth // peers
+    piece = angles // groups
+    moved = (cols // 2 + share // 2) * deep
+    sent = moved + piece + SUBS
+    f32 = jnp.float32
+    payload = pl.pallas_call(
+        functools.partial(pack_kernel, piece),
+        out_shape=jax.ShapeDtypeStruct((peers, sent, LANES), f32),
+        scratch_shapes=[pltpu.VMEM((angles, LANES), f32)],
+        name="pack",
+    )(volume, measured, weights, offsets)
+    arrived = lax.all_to_all(payload, ("gx", "gy"), 0, 0, tiled=True)
+    wide = taps * cols
+    dims = (bricks, groups, cols, taps, angles, share, deep)
+    payload = pl.pallas_call(
+        functools.partial(main_kernel, dims),
+        out_shape=jax.ShapeDtypeStruct((peers, moved + SUBS, LANES), f32),
+        scratch_shapes=[
+            pltpu.VMEM((bricks, 2 * angles, 2 * wide), jnp.bfloat16),
+            pltpu.VMEM((bricks, 2 * wide, 2 * angles), jnp.bfloat16),
+            pltpu.VMEM((bricks, angles, LANES), jnp.int32),
+            pltpu.VMEM((SUBS, LANES), f32),
+        ],
+        name="both_ways",
+    )(arrived)
+    arrived = lax.all_to_all(payload, ("gx", "gy"), 0, 0, tiled=True)
+    gradient, resid, square = pl.pallas_call(
+        unpack_kernel,
+        out_shape=(
+            jax.ShapeDtypeStruct(volume.shape, f32),
+            jax.ShapeDtypeStruct(measured.shape, f32),
+            jax.ShapeDtypeStruct((SUBS, LANES), f32),
+        ),
+        name="unpack",
+    )(arrived)
+    entries = angles * rows * depth * groups * lax.axis_size("gz")
+    misfit = jnp.sum(butterfly(square, "gz")) / entries
+    return gradient, resid, misfit
+
+
 def solution(mesh):
     in_specs = (P("gx", "gy", "gz"), P(None, None, "gx"), P(None, "gx"), P("gx", "gy", "gz"))
     out_specs = (P("gx", "gy", "gz"), P("gx", "gy", "gz"), P())

time: 491 us -> 91.3 us (0.19)
  local copies, waits for them, and re-layouts: 161 us -> 3.03 us
  other arithmetic: 120 us -> 1.28 us
  waiting for transfers between devices: 101 us -> 2.33 us
  matrix products: 44 us -> 0 us
  blocking collectives: 39 us -> 62.8 us
  Pallas kernels: 0 us -> 17.4 us
  between operations: 15.6 us -> 2.41 us
    add x9 -> x0, other arithmetic: 112 us -> none  [the longest x8 109 us: project_per_angle(): total = total + window[tap, tap:tap + 2 * rows]]
    all_to_all x0 -> x2, blocking collectives: none -> 62.8 us  [body(): arrived = lax.all_to_all(payload, ('gx', 'gy'), 0, 0, tiled=True)]
    gather x16 -> x0, local copies, waits for them, and re-layouts: 56.4 us -> none  [the longest x8 48.6 us: project_per_angle(): window = lax.dynamic_slice_in_dim(plane, shift, 2 * rows + taps - 1, 1)]
    ppermute x2 -> x1, waiting for transfers between devices: 52.8 us -> 2.33 us  [butterfly(): x = x + lax.ppermute(x, axis, [(i, i ^ step) for i in range(count)])]
    dot_general x16 -> x0, matrix products: 44 us -> none  [the longest x8 23.8 us: backward(): jnp.einsum('adc,adyz->cyz', wb, sheared, precision=lax.Precision.HIGHEST)]
    another operation x9 -> x0, local copies, waits for them, and re-layouts: 40.8 us -> none  [the longest x8 40.8 us: backward_per_angle(): jnp.stack([window[taps - 1 - tap:taps - 1 - tap + rows] for tap in range(...]
    psum x1 -> x0, blocking collectives: 39 us -> none  [body(): lax.psum(jnp.sum(resid_share * resid_share), ('gx', 'gy', 'gz')) / entries]
    reduce_scatter x1 -> x0, waiting for transfers between devices: 37.3 us -> none  [body(): lax.psum_scatter(partial_value, 'gx', scatter_dimension=0, tiled=True)]
  transfers between devices with their start and end apart: 5 -> 1, of which waited for: 4 -> 1; matrix products, arithmetic and copies ran while one was open for 0% -> 0% of each run, Pallas kernels for 0% -> 0%
where the time goes in v1:
time: 91.3 us; the launch traced here: 90.8 us
  blocking collectives  62.8 us (69%)
  Pallas kernels  17.4 us (19%)
  local copies, waits for them, and re-layouts  3.03 us (3%)
  between operations  2.41 us (3%)
  waiting for transfers between devices  2.33 us (3%)
  starting transfers between devices  1.49 us (2%)
  other arithmetic  1.28 us (1%)
    all_to_all x2, blocking collectives, body(): arrived = lax.all_to_all(payload, ('gx', 'gy'), 0, 0, tiled=True)  62.8 us
    pallas_call x1, Pallas kernels, body(): pl.pallas_call(functools.partial(main_kernel, dims), out_shape=jax.ShapeD...  12.5 us
    unnamed x2, local copies, waits for them, and re-layouts  3.03 us
    pallas_call x1, Pallas kernels, body(): pl.pallas_call(functools.partial(pack_kernel, piece), out_shape=jax.Shape...  2.63 us
    ppermute x1, waiting for transfers between devices, butterfly(): x = x + lax.ppermute(x, axis, [(i, i ^ step) for i in range(count)])  2.33 us
    pallas_call x1, Pallas kernels, body(): pl.pallas_call(unpack_kernel, out_shape=(jax.ShapeDtypeStruct(volume.shap...  2.23 us
  transfers between devices with their start and end apart: 1, of which 1 were waited for; matrix products, arithmetic and copies ran while one was open for 0% of the time, Pallas kernels for 0%

profile of v1, /device:TPU:0, one launch (start us, length us, event | category | flops | bytes accessed | tf_op | source)
XLA Modules:
  0.0 90.8 jit_solution(8630474986606045521)
XLA Ops:
  0.6 1.4 %copy.8.off_ref = s32[64,1]{1,0:T(8,128)} copy(s32[64,1]{0,1:T(1,128)} %param.6) | data formatting | bytes 512 | tf_op args[2]
  2.0 1.7 %copy.7.w_ref = f32[64,8,16]{2,1,0:T(8,128)} copy(f32[64,8,16]{0,2,1:T(8,128)} %param.5) | data formatting | bytes 65536 | tf_op args[1]
  3.7 2.6 %pack.1 = f32[16,136,128]{2,1,0:T(8,128)} custom-call(f32[16,64,128]{2,1,0:T(8,128)} %vol_ref.1, f32[8,64,128]{2,1,0:T(8,128)} %meas_ref.1, f32[64,8,16]{2,1,0:T(8,128)} %copy.7.w_ref, s32[64,1]{1,0:T(8,128)} %copy.8.off_ref), custom_call_target="tpu_custom_call" | custom-call | tf_op jit(solution)/shard_map/pack/pallas_call | solution.py:267
  6.3 36.2 %all_to_all.10.in_ref = f32[16,136,128]{2,1,0:T(8,128)} all-to-all(f32[16,136,128]{2,1,0:T(8,128)} %pack.1), channel_id=1, replica_groups=mesh['gx'=8,'gy'=2,'gz'=2] {'gx','gy'}, dimensions={0} | all-to-all | bytes 2228224 | tf_op jit(solution)/shard_map/all_to_all | solution.py:273
  42.5 12.5 %both_ways.1 = f32[16,104,128]{2,1,0:T(8,128)} custom-call(f32[16,136,128]{2,1,0:T(8,128)} %all_to_all.10.in_ref), custom_call_target="tpu_custom_call" | custom-call | tf_op jit(solution)/shard_map/both_ways/pallas_call | solution.py:276
  55.0 26.7 %all_to_all.11.in_ref = f32[16,104,128]{2,1,0:T(8,128)} all-to-all(f32[16,104,128]{2,1,0:T(8,128)} %both_ways.1), channel_id=1, replica_groups=mesh['gx'=8,'gy'=2,'gz'=2] {'gx','gy'}, dimensions={0} | all-to-all | bytes 1703936 | tf_op jit(solution)/shard_map/all_to_all | solution.py:287
  81.7 2.2 %unpack.1 = (f32[16,64,128]{2,1,0:T(8,128)}, f32[8,64,128]{2,1,0:T(8,128)}, f32[8,128]{1,0:T(8,128)}) custom-call(f32[16,104,128]{2,1,0:T(8,128)} %all_to_all.11.in_ref), custom_call_target="tpu_custom_call" | custom-call | tf_op jit(solution)/shard_map/unpack/pallas_call | solution.py:288
  83.9 1.5 %collective-permute-start = (f32[8,128]{1,0:T(8,128)}, f32[8,128]{1,0:T(8,128)S(1)}, u32[]{:S(2)}, u32[]{:S(2)}) collective-permute-start(f32[8,128]{1,0:T(8,128)} %get-tuple-element.8), channel_id=1, source_target_pairs={{0,1},{1,0},{2,3},{3,2},{4,5},{5,4},{6,7},{7,6},{8,9},{9,8},{10,11... | collective-permute-start | bytes 12296 | tf_op jit(solution)/shard_map/ppermute | solution.py:165
  85.4 2.3 %collective-permute-done = f32[8,128]{1,0:T(8,128)S(1)} collective-permute-done((f32[8,128]{1,0:T(8,128)}, f32[8,128]{1,0:T(8,128)S(1)}, u32[]{:S(2)}, u32[]{:S(2)}) %collective-permute-start) | collective-permute-done | bytes 4128 | tf_op jit(solution)/shard_map/ppermute | solution.py:165
  87.7 1.3 %add_reduce_fusion = f32[]{:T(128)} fusion(f32[8,128]{1,0:T(8,128)} %get-tuple-element.8, f32[8,128]{1,0:T(8,128)S(1)} %collective-permute-done), kind=kLoop, calls=%fused_computation | loop fusion | flops 2047 | bytes 8196 | tf_op jit(solution)/shard_map/reduce_sum | solution.py:298
Async XLA Ops:
  83.9 3.8 %collective-permute-start = (f32[8,128]{1,0:T(8,128)}, f32[8,128]{1,0:T(8,128)S(1)}, u32[]{:S(2)}, u32[]{:S(2)}) collective-permute-start(f32[8,128]{1,0:T(8,128)} %get-tuple-element.8), channel_id=1, source_target_pairs={{0,1},{1,0},{2,3},{3,2},{4,5},{5,4},{6,7},{7,6},{8,9},{9,8},{10,11... | collective-permute-start | bytes 12296 | tf_op jit(solution)/shard_map/ppermute | solution.py:165

commit v2 on v1

--- a/solution.py
+++ b/solution.py
@@ -33,7 +33,7 @@
 def pack_kernel(half_rows, vol_ref, meas_ref, w_ref, off_ref, out_ref, flat_ref):
     cols, rows, depth = vol_ref.shape
     share = meas_ref.shape[0]
-    angles, taps, _ = w_ref.shape
+    wide, angles = w_ref.shape
     peers = out_ref.shape[0]
     deep = depth // peers
     at = 0
@@ -42,15 +42,13 @@
             pair = jnp.concatenate([ref[j], ref[j + count]], axis=0)
             out_ref[:, at : at + deep, :] = pair.T.reshape(peers, deep, LANES)
             at += deep
-    for tap in range(taps):
-        flat_ref[:, tap * cols : (tap + 1) * cols] = w_ref[:, tap, :]
+    flat_ref[...] = w_ref[...].T
     start = pl.multiple_of(lax.axis_index("gy") * half_rows, SUBS)
     part = flat_ref[pl.ds(start, half_rows), :]
     out_ref[:, at : at + half_rows, :] = jnp.broadcast_to(part, (peers, half_rows, LANES))
     at += half_rows
-    shift = jnp.broadcast_to(off_ref[...].astype(jnp.float32), (angles, LANES))
-    shift = jnp.concatenate([shift, jnp.zeros((LANES - angles, LANES), jnp.float32)], axis=0)
-    out_ref[:, at : at + SUBS, :] = jnp.broadcast_to(shift.T[:SUBS], (peers, SUBS, LANES))
+    shift = jnp.concatenate([off_ref[...], jnp.zeros((1, LANES - angles), jnp.int32)], axis=1).astype(jnp.float32)
+    out_ref[:, at : at + SUBS, :] = jnp.broadcast_to(shift, (peers, SUBS, LANES))
 
 
 def main_kernel(dims, in_ref, out_ref, wf_ref, wb_ref, sh_ref, sq_ref):
@@ -140,7 +138,7 @@
         out_ref[p, m_end : m_end + SUBS, :] = sq_ref[...]
 
 
-def unpack_kernel(in_ref, grad_ref, res_ref, sq_ref):
+def unpack_kernel(in_ref, grad_ref, res_ref):
     peers = in_ref.shape[0]
     cols, rows, depth = grad_ref.shape
     share = res_ref.shape[0]
@@ -152,10 +150,6 @@
             ref[j] = both[:rows]
             ref[j + count] = both[rows:]
             at += deep
-    total = in_ref[0, at : at + SUBS, :]
-    for p in range(1, peers):
-        total = total + in_ref[p, at : at + SUBS, :]
-    sq_ref[...] = total
 
 
 def butterfly(x, axis):
@@ -269,7 +263,7 @@
         out_shape=jax.ShapeDtypeStruct((peers, sent, LANES), f32),
         scratch_shapes=[pltpu.VMEM((angles, LANES), f32)],
         name="pack",
-    )(volume, measured, weights, offsets)
+    )(volume, measured, weights.transpose(1, 2, 0).reshape(taps * cols, angles), offsets.reshape(1, angles))
     arrived = lax.all_to_all(payload, ("gx", "gy"), 0, 0, tiled=True)
     wide = taps * cols
     dims = (bricks, groups, cols, taps, angles, share, deep)
@@ -285,17 +279,15 @@
         name="both_ways",
     )(arrived)
     arrived = lax.all_to_all(payload, ("gx", "gy"), 0, 0, tiled=True)
-    gradient, resid, square = pl.pallas_call(
+    square = butterfly(jnp.sum(arrived[:, moved:]), "gz")
+    gradient, resid = pl.pallas_call(
         unpack_kernel,
-        out_shape=(
-            jax.ShapeDtypeStruct(volume.shape, f32),
-            jax.ShapeDtypeStruct(measured.shape, f32),
-            jax.ShapeDtypeStruct((SUBS, LANES), f32),
-        ),
+        out_shape=(jax.ShapeDtypeStruct(volume.shape, f32), jax.ShapeDtypeStruct(measured.shape, f32)),
+        cost_estimate=pl.CostEstimate(flops=1 << 24, bytes_accessed=1 << 21, transcendentals=0),
         name="unpack",
     )(arrived)
     entries = angles * rows * depth * groups * lax.axis_size("gz")
-    misfit = jnp.sum(butterfly(square, "gz")) / entries
+    misfit = square / entries
     return gradient, resid, misfit
 
 

time: 91.3 us -> 85 us (0.931)
  local copies, waits for them, and re-layouts: 3.03 us -> 0.01 us
  waiting for transfers between devices: 2.33 us -> 0.01 us
    unnamed x2, local copies, waits for them, and re-layouts: 3.03 us -> 0.01 us
    ppermute x1, waiting for transfers between devices: 2.33 us -> 0.01 us  [butterfly(): x = x + lax.ppermute(x, axis, [(i, i ^ step) for i in range(count)])]
  transfers between devices with their start and end apart: 1 -> 1, of which waited for: 1 -> 0; matrix products, arithmetic and copies ran while one was open for 0% -> 0% of each run, Pallas kernels for 0% -> 3%
where the time goes in v2:
time: 85 us; the launch traced here: 84.6 us
  blocking collectives  62.1 us (73%)
  Pallas kernels  17.2 us (20%)
  between operations  3.03 us (4%)
  starting transfers between devices  1.49 us (2%)
    all_to_all x2, blocking collectives, body(): arrived = lax.all_to_all(payload, ('gx', 'gy'), 0, 0, tiled=True)  62.1 us
    pallas_call x1, Pallas kernels, body(): pl.pallas_call(functools.partial(main_kernel, dims), out_shape=jax.ShapeD...  12.5 us
    pallas_call x1, Pallas kernels, body(): pl.pallas_call(functools.partial(pack_kernel, piece), out_shape=jax.Shape...  2.48 us
    pallas_call x1, Pallas kernels, body(): pl.pallas_call(unpack_kernel, out_shape=(jax.ShapeDtypeStruct(volume.shap...  2.23 us
  transfers between devices with their start and end apart: 1, of which 0 were waited for; matrix products, arithmetic and copies ran while one was open for 0% of the time, Pallas kernels for 3%

profile of v2, /device:TPU:0, one launch (start us, length us, event | category | flops | bytes accessed | tf_op | source)
XLA Modules:
  0.0 84.6 jit_solution(2159396576504032787)
XLA Ops:
  0.6 2.5 %pack.1 = f32[16,136,128]{2,1,0:T(8,128)} custom-call(f32[16,64,128]{2,1,0:T(8,128)} %vol_ref.1, f32[8,64,128]{2,1,0:T(8,128)} %meas_ref.1, f32[128,64]{1,0:T(8,128)} %bitcast.4, s32[1,64]{1,0:T(1,128)} %bitcast.5), custom_call_target="tpu_custom_call" | custom-call | tf_op jit(solution)/shard_map/pack/pallas_call | solution.py:261
  3.1 36.2 %all_to_all.10.in_ref = f32[16,136,128]{2,1,0:T(8,128)} all-to-all(f32[16,136,128]{2,1,0:T(8,128)} %pack.1), channel_id=1, replica_groups=mesh['gx'=8,'gy'=2,'gz'=2] {'gx','gy'}, dimensions={0} | all-to-all | bytes 2228224 | tf_op jit(solution)/shard_map/all_to_all | solution.py:267
  39.3 12.5 %both_ways.1 = f32[16,104,128]{2,1,0:T(8,128)} custom-call(f32[16,136,128]{2,1,0:T(8,128)} %all_to_all.10.in_ref), custom_call_target="tpu_custom_call" | custom-call | tf_op jit(solution)/shard_map/both_ways/pallas_call | solution.py:270
  51.8 26.0 %all_to_all.11.in_ref = f32[16,104,128]{2,1,0:T(8,128)S(1)} all-to-all(f32[16,104,128]{2,1,0:T(8,128)} %both_ways.1), channel_id=1, replica_groups=mesh['gx'=8,'gy'=2,'gz'=2] {'gx','gy'}, dimensions={0} | all-to-all | bytes 1703936 | tf_op jit(solution)/shard_map/all_to_all | solution.py:281
  77.8 0.0 copy-start
  77.8 0.7 slice_reduce_fusion
  78.5 1.5 %collective-permute-start = (f32[]{:T(128)}, f32[]{:T(128)}, u32[]{:S(2)}, u32[]{:S(2)}) collective-permute-start(f32[]{:T(128)} %slice_reduce_fusion), channel_id=1, source_target_pairs={{0,1},{1,0},{2,3},{3,2},{4,5},{5,4},{6,7},{7,6},{8,9},{9,8},{10,11... | collective-permute-start | bytes 20 | tf_op jit(solution)/shard_map/ppermute | solution.py:159
  80.0 0.0 copy-done
  80.0 2.2 %unpack.1 = (f32[16,64,128]{2,1,0:T(8,128)}, f32[8,64,128]{2,1,0:T(8,128)}) custom-call(f32[16,104,128]{2,1,0:T(8,128)} %copy-done), custom_call_target="tpu_custom_call" | custom-call | flops 16777216 | bytes 2097152 | tf_op jit(solution)/shard_map/unpack/pallas_call | solution.py:283
  82.2 0.0 collective-permute-done
Async XLA Ops:
  77.8 2.2 %copy-start = (f32[16,104,128]{2,1,0:T(8,128)}, f32[16,104,128]{2,1,0:T(8,128)S(1)}, u32[]{:S(2)}) copy-start(f32[16,104,128]{2,1,0:T(8,128)S(1)} %all_to_all.11.in_ref) | copy-start | bytes 2555908
  78.5 3.7 %collective-permute-start = (f32[]{:T(128)}, f32[]{:T(128)}, u32[]{:S(2)}, u32[]{:S(2)}) collective-permute-start(f32[]{:T(128)} %slice_reduce_fusion), channel_id=1, source_target_pairs={{0,1},{1,0},{2,3},{3,2},{4,5},{5,4},{6,7},{7,6},{8,9},{9,8},{10,11... | collective-permute-start | bytes 20 | tf_op jit(solution)/shard_map/ppermute | solution.py:159

commit v3 on v2

--- a/solution.py
+++ b/solution.py
@@ -9,6 +9,8 @@
 
 LANES = 128
 SUBS = 8
+STRIDE = 72
+TOGETHER = 2
 
 
 def split(x):
@@ -51,91 +53,172 @@
     out_ref[:, at : at + SUBS, :] = jnp.broadcast_to(shift, (peers, SUBS, LANES))
 
 
-def main_kernel(dims, in_ref, out_ref, wf_ref, wb_ref, sh_ref, sq_ref):
+def three(x):
+    high, low = split(x)
+    return jnp.concatenate([high, low, high], axis=0)
+
+
+def main_kernel(dims, in_hbm, out_hbm, *scratch):
+    in_ref, out_ref, wf_ref, wb_ref, row_ref, int_ref, sh_ref, total_ref = scratch[:8]
+    turn_refs, (in_sem, row_sem, sh_sem, out_sem) = scratch[8 : 8 + TOGETHER], scratch[8 + TOGETHER :]
     bricks, groups, cols, taps, angles, share, deep = dims
     wide = taps * cols
     piece = angles // groups
-    w_at = (cols // 2 + share // 2) * deep
+    half, quarter = cols // 2, share // 2
+    m_at = half * deep
+    w_at = m_at + quarter * deep
     s_at = w_at + piece
-    m_at = (cols // 2) * deep
-    quarter = share // 2
-    for i in range(bricks):
+
+    def from_brick(i):
+        return pltpu.make_async_copy(
+            in_hbm.at[pl.ds(i * groups, groups)], in_ref.at[pl.ds(i * groups, groups)], in_sem.at[i]
+        )
+
+    def shifts_of(i):
+        return pltpu.make_async_copy(in_hbm.at[i * groups, pl.ds(s_at, SUBS), :], row_ref.at[i], row_sem.at[i])
+
+    def to_brick(i):
+        return pltpu.make_async_copy(
+            out_ref.at[pl.ds(i * groups, groups)], out_hbm.at[pl.ds(i * groups, groups)], out_sem.at[i]
+        )
+
+    for i in range(bricks):
+        shifts_of(i).start()
+    for i in range(bricks):
+        from_brick(i).start()
+    total_ref[...] = jnp.zeros_like(total_ref)
+    for i in range(bricks):
+        shifts_of(i).wait()
+        int_ref[i : i + 1, :] = row_ref[i, :1, :].astype(jnp.int32)
+    to_scalars = pltpu.make_async_copy(int_ref, sh_ref, sh_sem)
+    to_scalars.start()
+    lane_c = lane_ids(cols)
+    lane = lane_ids(deep)
+    zero = jnp.zeros((cols, LANES), jnp.bfloat16)
+
+    def shift_of(i, a):
+        return sh_ref[i, a]
+
+    def weights_of(i):
         w = jnp.concatenate([in_ref[i * groups + h, w_at : w_at + piece, :] for h in range(groups)], axis=0)
         high, low = split(w)
-        wf_ref[i, :angles, :wide] = high
-        wf_ref[i, :angles, wide:] = high
-        wf_ref[i, angles:, :wide] = low
-        wf_ref[i, angles:, wide:] = jnp.zeros_like(low)
+        wf_ref[i, :, :wide] = high
+        wf_ref[i, :, wide : 2 * wide] = high
+        wf_ref[i, :, 2 * wide :] = low
         high, low = split(w.T)
-        wb_ref[i, :wide, :angles] = high
-        wb_ref[i, :wide, angles:] = high
-        wb_ref[i, wide:, :angles] = low
-        wb_ref[i, wide:, angles:] = jnp.zeros_like(low)
-        row = in_ref[i * groups, s_at : s_at + SUBS, :]
-        sh_ref[i] = jnp.concatenate([row] * (LANES // SUBS), axis=0).T[:angles].astype(jnp.int32)
-    sq_ref[...] = jnp.zeros_like(sq_ref)
-    lane_a = lane_ids(angles)
-    lane_c = lane_ids(cols)
-
-    def pair_of_depths(q, carry):
-        zs = [2 * q, 2 * q + 1]
-        accs = [jnp.zeros((angles, LANES), jnp.float32) for _ in zs]
-        for i in range(bricks):
+        wb_ref[i, :, :angles] = high
+        wb_ref[i, :, angles : 2 * angles] = high
+        wb_ref[i, :, 2 * angles :] = low
+
+    def project(i, turn_ref):
+        for q in range(deep // 2):
             blocks = []
-            for z in zs:
-                first, second = (in_ref[i * groups + h, pl.ds(z, cols // 2, stride=deep), :] for h in range(2))
+            for z in (2 * q, 2 * q + 1):
+                first, second = (in_ref[i * groups + h, pl.ds(z, half, stride=deep), :] for h in range(2))
                 x = jnp.concatenate(unpair(first, second), axis=0)
-                moved = [x]
-                for tap in range(1, taps):
-                    moved.append(jnp.where(lane_c < LANES - tap, pltpu.roll(x, LANES - tap, 1), 0.0))
-                blocks.append(jnp.concatenate(split(jnp.concatenate(moved, axis=0)), axis=0))
+                parts = []
+                for part in split(x):
+                    moved = [part]
+                    for tap in range(1, taps):
+                        moved.append(jnp.where(lane_c < LANES - tap, pltpu.roll(part, LANES - tap, 1), zero))
+                    parts.append(jnp.concatenate(moved, axis=0))
+                high, low = parts
+                blocks.append(jnp.concatenate([high, low, high], axis=0))
             out = jnp.dot(wf_ref[i], jnp.concatenate(blocks, axis=1), preferred_element_type=jnp.float32)
-            out = out[:angles] + out[angles:]
-            reach = lane_a + sh_ref[i]
-            index = reach & (LANES - 1)
             for k in range(2):
-                part = out[:, k * LANES : (k + 1) * LANES]
-                part = jnp.take_along_axis(part, index, axis=1, mode="promise_in_bounds")
-                accs[k] = accs[k] + jnp.where(reach < LANES, part, 0.0)
-        resids = []
-        for k, z in enumerate(zs):
-            rows = []
-            for i in range(bricks):
-                first, second = (in_ref[i * groups + h, pl.ds(m_at + z, quarter, stride=deep), :] for h in range(2))
-                rows.extend(unpair(first, second))
-            resid = accs[k] - jnp.concatenate(rows, axis=0)
-            square = resid * resid
-            for at in range(0, angles, SUBS):
-                sq_ref[...] += square[at : at + SUBS]
-            resids.append(resid)
-            for i in range(bricks):
-                low = resid[i * share : i * share + quarter]
-                high = resid[i * share + quarter : (i + 1) * share]
-                for h, block in enumerate(unpair(low, high)):
-                    out_ref[i * groups + h, pl.ds(m_at + z, quarter, stride=deep), :] = block
-        for i in range(bricks):
-            back = lane_a - sh_ref[i]
-            index = back & (LANES - 1)
-            blocks = []
-            for k in range(2):
-                part = jnp.take_along_axis(resids[k], index, axis=1, mode="promise_in_bounds")
-                part = jnp.where(back >= 0, part, 0.0)
-                blocks.append(jnp.concatenate(split(part), axis=0))
+                at = (2 * q + k) * STRIDE
+                turn_ref[at : at + angles, :] = out[:, k * LANES : (k + 1) * LANES]
+
+    def gather_rows(i, turn_refs):
+        for a in range(angles):
+            part = total_ref[a]
+            for k, turn_ref in enumerate(turn_refs):
+                shift = shift_of(i + k, a)
+                moved = pltpu.roll(turn_ref[pl.ds(a, deep, stride=STRIDE), :], LANES - shift, 1)
+                part = part + jnp.where(lane < LANES - shift, moved, 0.0)
+            total_ref[a] = part
+
+    def forward(n, carry):
+        i = n * TOGETHER
+        for k, turn_ref in enumerate(turn_refs):
+            from_brick(i + k).wait()
+            weights_of(i + k)
+            project(i + k, turn_ref)
+
+        @pl.when(n == 0)
+        def _():
+            to_scalars.wait()
+
+        gather_rows(i, turn_refs)
+        return carry
+
+    def scatter_rows(i, turn_ref):
+        for a in range(angles):
+            shift = shift_of(i, a)
+            turn_ref[pl.ds(a, deep, stride=STRIDE), :] = jnp.where(lane >= shift, pltpu.roll(total_ref[a], shift, 1), 0.0)
+
+    def backproject(i, turn_ref):
+        for q in range(deep // 2):
+            zs = (2 * q, 2 * q + 1)
+            blocks = [three(turn_ref[z * STRIDE : z * STRIDE + angles, :]) for z in zs]
             out = jnp.dot(wb_ref[i], jnp.concatenate(blocks, axis=1), preferred_element_type=jnp.float32)
-            out = out[:wide] + out[wide:]
             for k, z in enumerate(zs):
                 part = out[:, k * LANES : (k + 1) * LANES]
                 total = part[:cols]
                 for tap in range(1, taps):
                     total = total + jnp.where(lane_c >= tap, pltpu.roll(part[tap * cols : (tap + 1) * cols], tap, 1), 0.0)
-                for h, block in enumerate(unpair(total[: cols // 2], total[cols // 2 :])):
-                    out_ref[i * groups + h, pl.ds(z, cols // 2, stride=deep), :] = block
+                for h, block in enumerate(unpair(total[:half], total[half:])):
+                    out_ref[i * groups + h, pl.ds(z, half, stride=deep), :] = block
+
+    def backward(n, carry):
+        i = n * TOGETHER
+        for k, turn_ref in enumerate(turn_refs):
+            scatter_rows(i + k, turn_ref)
+        for k, turn_ref in enumerate(turn_refs):
+            backproject(i + k, turn_ref)
+        for k in range(TOGETHER):
+            to_brick(i + k).start()
         return carry
 
-    lax.fori_loop(0, deep // 2, pair_of_depths, 0)
-    m_end = m_at + quarter * deep
+    lax.fori_loop(0, bricks // TOGETHER, forward, 0)
+    square = jnp.zeros((deep, LANES), jnp.float32)
+    for i in range(bricks):
+        for j in range(quarter):
+            at = m_at + j * deep
+            low_at, high_at = i * share + j, i * share + quarter + j
+            low, high = unpair(*(in_ref[i * groups + h, at : at + deep, :] for h in range(2)))
+            low, high = total_ref[low_at] - low, total_ref[high_at] - high
+            total_ref[low_at], total_ref[high_at] = low, high
+            square = square + low * low + high * high
+            for h, block in enumerate(unpair(low, high)):
+                out_ref[i * groups + h, at : at + deep, :] = block
     for p in range(bricks * groups):
-        out_ref[p, m_end : m_end + SUBS, :] = sq_ref[...]
+        out_ref[p, w_at : w_at + deep, :] = square
+    lax.fori_loop(0, bricks // TOGETHER, backward, 0)
+    for i in range(bricks):
+        to_brick(i).wait()
+
+
+def main_scratch(dims):
+    bricks, groups, cols, taps, angles, share, deep = dims
+    wide = taps * cols
+    f32, bf16 = jnp.float32, jnp.bfloat16
+    rows = (cols // 2 + share // 2) * deep
+    return [
+        pltpu.VMEM((bricks * groups, rows + angles // groups + SUBS, LANES), f32),
+        pltpu.VMEM((bricks * groups, rows + SUBS, LANES), f32),
+        pltpu.VMEM((bricks, angles, 3 * wide), bf16),
+        pltpu.VMEM((bricks, wide, 3 * angles), bf16),
+        pltpu.VMEM((bricks, SUBS, LANES), f32),
+        pltpu.VMEM((bricks, LANES), jnp.int32),
+        pltpu.SMEM((bricks, LANES), jnp.int32),
+        pltpu.VMEM((angles, deep, LANES), f32),
+        *[pltpu.VMEM((deep * STRIDE, LANES), f32) for _ in range(TOGETHER)],
+        pltpu.SemaphoreType.DMA((bricks,)),
+        pltpu.SemaphoreType.DMA((bricks,)),
+        pltpu.SemaphoreType.DMA,
+        pltpu.SemaphoreType.DMA((bricks,)),
+    ]
 
 
 def unpack_kernel(in_ref, grad_ref, res_ref):
@@ -265,17 +348,13 @@
         name="pack",
     )(volume, measured, weights.transpose(1, 2, 0).reshape(taps * cols, angles), offsets.reshape(1, angles))
     arrived = lax.all_to_all(payload, ("gx", "gy"), 0, 0, tiled=True)
-    wide = taps * cols
     dims = (bricks, groups, cols, taps, angles, share, deep)
     payload = pl.pallas_call(
         functools.partial(main_kernel, dims),
         out_shape=jax.ShapeDtypeStruct((peers, moved + SUBS, LANES), f32),
-        scratch_shapes=[
-            pltpu.VMEM((bricks, 2 * angles, 2 * wide), jnp.bfloat16),
-            pltpu.VMEM((bricks, 2 * wide, 2 * angles), jnp.bfloat16),
-            pltpu.VMEM((bricks, angles, LANES), jnp.int32),
-            pltpu.VMEM((SUBS, LANES), f32),
-        ],
+        in_specs=[pl.BlockSpec(memory_space=pl.ANY)],
+        out_specs=pl.BlockSpec(memory_space=pl.ANY),
+        scratch_shapes=main_scratch(dims),
         name="both_ways",
     )(arrived)
     arrived = lax.all_to_all(payload, ("gx", "gy"), 0, 0, tiled=True)

time: 85 us -> 82.2 us (0.967)
  Pallas kernels: 17.2 us -> 14.4 us
    pallas_call x1, Pallas kernels: 12.5 us -> 9.71 us  [body(): pl.pallas_call(functools.partial(main_kernel, dims), out_shape=jax.ShapeD...]
where the time goes in v3:
time: 82.2 us; the launch traced here: 81.8 us
  blocking collectives  62.1 us (76%)
  Pallas kernels  14.4 us (18%)
  between operations  3.04 us (4%)
  starting transfers between devices  1.49 us (2%)
    all_to_all x2, blocking collectives, body(): arrived = lax.all_to_all(payload, ('gx', 'gy'), 0, 0, tiled=True)  62.1 us
    pallas_call x1, Pallas kernels, body(): pl.pallas_call(functools.partial(main_kernel, dims), out_shape=jax.ShapeD...  9.71 us
    pallas_call x1, Pallas kernels, body(): pl.pallas_call(functools.partial(pack_kernel, piece), out_shape=jax.Shape...  2.48 us
    pallas_call x1, Pallas kernels, body(): pl.pallas_call(unpack_kernel, out_shape=(jax.ShapeDtypeStruct(volume.shap...  2.23 us
  transfers between devices with their start and end apart: 1, of which 0 were waited for; matrix products, arithmetic and copies ran while one was open for 0% of the time, Pallas kernels for 3%

profile of v3, /device:TPU:0, one launch (start us, length us, event | category | flops | bytes accessed | tf_op | source)
XLA Modules:
  0.0 81.8 jit_solution(9796258352568327745)
XLA Ops:
  0.6 2.5 %pack.1 = f32[16,136,128]{2,1,0:T(8,128)} custom-call(f32[16,64,128]{2,1,0:T(8,128)} %vol_ref.1, f32[8,64,128]{2,1,0:T(8,128)} %meas_ref.1, f32[128,64]{1,0:T(8,128)} %bitcast.4, s32[1,64]{1,0:T(1,128)} %bitcast.5), custom_call_target="tpu_custom_call" | custom-call | tf_op jit(solution)/shard_map/pack/pallas_call | solution.py:344
  3.1 36.2 %all_to_all.10.in_hbm = f32[16,136,128]{2,1,0:T(8,128)} all-to-all(f32[16,136,128]{2,1,0:T(8,128)} %pack.1), channel_id=1, replica_groups=mesh['gx'=8,'gy'=2,'gz'=2] {'gx','gy'}, dimensions={0} | all-to-all | bytes 2228224 | tf_op jit(solution)/shard_map/all_to_all | solution.py:350
  39.3 9.7 %both_ways.1 = f32[16,104,128]{2,1,0:T(8,128)} custom-call(f32[16,136,128]{2,1,0:T(8,128)} %all_to_all.10.in_hbm), custom_call_target="tpu_custom_call" | custom-call | tf_op jit(solution)/shard_map/both_ways/pallas_call | solution.py:352
  49.0 26.0 %all_to_all.11.in_ref = f32[16,104,128]{2,1,0:T(8,128)S(1)} all-to-all(f32[16,104,128]{2,1,0:T(8,128)} %both_ways.1), channel_id=1, replica_groups=mesh['gx'=8,'gy'=2,'gz'=2] {'gx','gy'}, dimensions={0} | all-to-all | bytes 1703936 | tf_op jit(solution)/shard_map/all_to_all | solution.py:360
  75.0 0.0 copy-start
  75.0 0.7 slice_reduce_fusion
  75.7 1.5 %collective-permute-start = (f32[]{:T(128)}, f32[]{:T(128)}, u32[]{:S(2)}, u32[]{:S(2)}) collective-permute-start(f32[]{:T(128)} %slice_reduce_fusion), channel_id=1, source_target_pairs={{0,1},{1,0},{2,3},{3,2},{4,5},{5,4},{6,7},{7,6},{8,9},{9,8},{10,11... | collective-permute-start | bytes 20 | tf_op jit(solution)/shard_map/ppermute | solution.py:242
  77.2 0.0 copy-done
  77.2 2.2 %unpack.1 = (f32[16,64,128]{2,1,0:T(8,128)}, f32[8,64,128]{2,1,0:T(8,128)}) custom-call(f32[16,104,128]{2,1,0:T(8,128)} %copy-done), custom_call_target="tpu_custom_call" | custom-call | flops 16777216 | bytes 2097152 | tf_op jit(solution)/shard_map/unpack/pallas_call | solution.py:362
  79.4 0.0 collective-permute-done
Async XLA Ops:
  75.0 2.2 %copy-start = (f32[16,104,128]{2,1,0:T(8,128)}, f32[16,104,128]{2,1,0:T(8,128)S(1)}, u32[]{:S(2)}) copy-start(f32[16,104,128]{2,1,0:T(8,128)S(1)} %all_to_all.11.in_ref) | copy-start | bytes 2555908
  75.7 3.7 %collective-permute-start = (f32[]{:T(128)}, f32[]{:T(128)}, u32[]{:S(2)}, u32[]{:S(2)}) collective-permute-start(f32[]{:T(128)} %slice_reduce_fusion), channel_id=1, source_target_pairs={{0,1},{1,0},{2,3},{3,2},{4,5},{5,4},{6,7},{7,6},{8,9},{9,8},{10,11... | collective-permute-start | bytes 20 | tf_op jit(solution)/shard_map/ppermute | solution.py:242

commit v4 on v3

--- a/solution.py
+++ b/solution.py
@@ -58,9 +58,9 @@
     return jnp.concatenate([high, low, high], axis=0)
 
 
-def main_kernel(dims, in_hbm, out_hbm, *scratch):
-    in_ref, out_ref, wf_ref, wb_ref, row_ref, int_ref, sh_ref, total_ref = scratch[:8]
-    turn_refs, (in_sem, row_sem, sh_sem, out_sem) = scratch[8 : 8 + TOGETHER], scratch[8 + TOGETHER :]
+def main_kernel(dims, in_ref, out_ref, *scratch):
+    wf_ref, wb_ref, int_ref, sh_ref, total_ref = scratch[:5]
+    turn_refs, sh_sem = scratch[5 : 5 + TOGETHER], scratch[5 + TOGETHER]
     bricks, groups, cols, taps, angles, share, deep = dims
     wide = taps * cols
     piece = angles // groups
@@ -69,35 +69,16 @@
     w_at = m_at + quarter * deep
     s_at = w_at + piece
 
-    def from_brick(i):
-        return pltpu.make_async_copy(
-            in_hbm.at[pl.ds(i * groups, groups)], in_ref.at[pl.ds(i * groups, groups)], in_sem.at[i]
-        )
-
-    def shifts_of(i):
-        return pltpu.make_async_copy(in_hbm.at[i * groups, pl.ds(s_at, SUBS), :], row_ref.at[i], row_sem.at[i])
-
-    def to_brick(i):
-        return pltpu.make_async_copy(
-            out_ref.at[pl.ds(i * groups, groups)], out_hbm.at[pl.ds(i * groups, groups)], out_sem.at[i]
-        )
-
     for i in range(bricks):
-        shifts_of(i).start()
-    for i in range(bricks):
-        from_brick(i).start()
-    total_ref[...] = jnp.zeros_like(total_ref)
-    for i in range(bricks):
-        shifts_of(i).wait()
-        int_ref[i : i + 1, :] = row_ref[i, :1, :].astype(jnp.int32)
+        row = in_ref[i * groups, s_at : s_at + 1, :].astype(jnp.int32)
+        int_ref[i : i + 1, :] = row
+        int_ref[bricks + i : bricks + i + 1, :] = LANES - row
     to_scalars = pltpu.make_async_copy(int_ref, sh_ref, sh_sem)
     to_scalars.start()
+    total_ref[...] = jnp.zeros_like(total_ref)
     lane_c = lane_ids(cols)
     lane = lane_ids(deep)
     zero = jnp.zeros((cols, LANES), jnp.bfloat16)
-
-    def shift_of(i, a):
-        return sh_ref[i, a]
 
     def weights_of(i):
         w = jnp.concatenate([in_ref[i * groups + h, w_at : w_at + piece, :] for h in range(groups)], axis=0)
@@ -133,15 +114,14 @@
         for a in range(angles):
             part = total_ref[a]
             for k, turn_ref in enumerate(turn_refs):
-                shift = shift_of(i + k, a)
-                moved = pltpu.roll(turn_ref[pl.ds(a, deep, stride=STRIDE), :], LANES - shift, 1)
-                part = part + jnp.where(lane < LANES - shift, moved, 0.0)
+                reach = sh_ref[bricks + i + k, a]
+                moved = pltpu.roll(turn_ref[pl.ds(a, deep, stride=STRIDE), :], reach, 1)
+                part = part + jnp.where(lane < reach, moved, 0.0)
             total_ref[a] = part
 
     def forward(n, carry):
         i = n * TOGETHER
         for k, turn_ref in enumerate(turn_refs):
-            from_brick(i + k).wait()
             weights_of(i + k)
             project(i + k, turn_ref)
 
@@ -154,7 +134,7 @@
 
     def scatter_rows(i, turn_ref):
         for a in range(angles):
-            shift = shift_of(i, a)
+            shift = sh_ref[i, a]
             turn_ref[pl.ds(a, deep, stride=STRIDE), :] = jnp.where(lane >= shift, pltpu.roll(total_ref[a], shift, 1), 0.0)
 
     def backproject(i, turn_ref):
@@ -176,8 +156,6 @@
             scatter_rows(i + k, turn_ref)
         for k, turn_ref in enumerate(turn_refs):
             backproject(i + k, turn_ref)
-        for k in range(TOGETHER):
-            to_brick(i + k).start()
         return carry
 
     lax.fori_loop(0, bricks // TOGETHER, forward, 0)
@@ -195,29 +173,20 @@
     for p in range(bricks * groups):
         out_ref[p, w_at : w_at + deep, :] = square
     lax.fori_loop(0, bricks // TOGETHER, backward, 0)
-    for i in range(bricks):
-        to_brick(i).wait()
 
 
 def main_scratch(dims):
     bricks, groups, cols, taps, angles, share, deep = dims
     wide = taps * cols
     f32, bf16 = jnp.float32, jnp.bfloat16
-    rows = (cols // 2 + share // 2) * deep
     return [
-        pltpu.VMEM((bricks * groups, rows + angles // groups + SUBS, LANES), f32),
-        pltpu.VMEM((bricks * groups, rows + SUBS, LANES), f32),
         pltpu.VMEM((bricks, angles, 3 * wide), bf16),
         pltpu.VMEM((bricks, wide, 3 * angles), bf16),
-        pltpu.VMEM((bricks, SUBS, LANES), f32),
-        pltpu.VMEM((bricks, LANES), jnp.int32),
-        pltpu.SMEM((bricks, LANES), jnp.int32),
+        pltpu.VMEM((2 * bricks, LANES), jnp.int32),
+        pltpu.SMEM((2 * bricks, LANES), jnp.int32),
         pltpu.VMEM((angles, deep, LANES), f32),
         *[pltpu.VMEM((deep * STRIDE, LANES), f32) for _ in range(TOGETHER)],
-        pltpu.SemaphoreType.DMA((bricks,)),
-        pltpu.SemaphoreType.DMA((bricks,)),
         pltpu.SemaphoreType.DMA,
-        pltpu.SemaphoreType.DMA((bricks,)),
     ]
 
 
@@ -233,6 +202,10 @@
             ref[j] = both[:rows]
             ref[j + count] = both[rows:]
             at += deep
+
+
+def on_chip(x):
+    return pltpu.with_memory_space_constraint(x, pltpu.VMEM)
 
 
 def butterfly(x, axis):
@@ -343,7 +316,7 @@
     f32 = jnp.float32
     payload = pl.pallas_call(
         functools.partial(pack_kernel, piece),
-        out_shape=jax.ShapeDtypeStruct((peers, sent, LANES), f32),
+        out_shape=pltpu.VMEM((peers, sent, LANES), f32),
         scratch_shapes=[pltpu.VMEM((angles, LANES), f32)],
         name="pack",
     )(volume, measured, weights.transpose(1, 2, 0).reshape(taps * cols, angles), offsets.reshape(1, angles))
@@ -351,12 +324,10 @@
     dims = (bricks, groups, cols, taps, angles, share, deep)
     payload = pl.pallas_call(
         functools.partial(main_kernel, dims),
-        out_shape=jax.ShapeDtypeStruct((peers, moved + SUBS, LANES), f32),
-        in_specs=[pl.BlockSpec(memory_space=pl.ANY)],
-        out_specs=pl.BlockSpec(memory_space=pl.ANY),
+        out_shape=pltpu.VMEM((peers, moved + SUBS, LANES), f32),
         scratch_shapes=main_scratch(dims),
         name="both_ways",
-    )(arrived)
+    )(on_chip(arrived))
     arrived = lax.all_to_all(payload, ("gx", "gy"), 0, 0, tiled=True)
     square = butterfly(jnp.sum(arrived[:, moved:]), "gz")
     gradient, resid = pl.pallas_call(
@@ -364,7 +335,7 @@
         out_shape=(jax.ShapeDtypeStruct(volume.shape, f32), jax.ShapeDtypeStruct(measured.shape, f32)),
         cost_estimate=pl.CostEstimate(flops=1 << 24, bytes_accessed=1 << 21, transcendentals=0),
         name="unpack",
-    )(arrived)
+    )(on_chip(arrived))
     entries = angles * rows * depth * groups * lax.axis_size("gz")
     misfit = square / entries
     return gradient, resid, misfit

time: 82.2 us -> 76.9 us (0.936)
  Pallas kernels: 14.4 us -> 9.36 us
  blocking collectives: 62.1 us -> 61 us
  waiting for transfers between devices: 0.01 us -> 1.09 us
    pallas_call x2, Pallas kernels: 12.2 us -> 8.28 us  [the longest x1 6.85 us: body(): pl.pallas_call(functools.partial(main_kernel, dims), out_shape=pltpu.VMEM...]
    pallas_call x1, Pallas kernels: 2.23 us -> 1.08 us  [body(): pl.pallas_call(unpack_kernel, out_shape=(jax.ShapeDtypeStruct(volume.shap...]
    all_to_all x2, blocking collectives: 62.1 us -> 61 us  [body(): arrived = lax.all_to_all(payload, ('gx', 'gy'), 0, 0, tiled=True)]
    ppermute x1, waiting for transfers between devices: 0.01 us -> 1.09 us  [butterfly(): x = x + lax.ppermute(x, axis, [(i, i ^ step) for i in range(count)])]
  transfers between devices with their start and end apart: 1 -> 1, of which waited for: 0 -> 1; matrix products, arithmetic and copies ran while one was open for 0% -> 0% of each run, Pallas kernels for 3% -> 1%
where the time goes in v4:
time: 76.9 us; the launch traced here: 76.7 us
  blocking collectives  61 us (79%)
  Pallas kernels  9.36 us (12%)
  between operations  3.12 us (4%)
  starting transfers between devices  1.49 us (2%)
  waiting for transfers between devices  1.09 us (1%)
    all_to_all x2, blocking collectives, body(): arrived = lax.all_to_all(payload, ('gx', 'gy'), 0, 0, tiled=True)  61 us
    pallas_call x1, Pallas kernels, body(): pl.pallas_call(functools.partial(main_kernel, dims), out_shape=pltpu.VMEM...  6.85 us
  transfers between devices with their start and end apart: 1, of which 1 were waited for; matrix products, arithmetic and copies ran while one was open for 0% of the time, Pallas kernels for 1%

profile of v4, /device:TPU:0, one launch (start us, length us, event | category | flops | bytes accessed | tf_op | source)
XLA Modules:
  0.0 76.7 jit_solution(7788107583955095035)
XLA Ops:
  0.6 1.4 %pack.1 = f32[16,136,128]{2,1,0:T(8,128)S(1)} custom-call(f32[16,64,128]{2,1,0:T(8,128)} %vol_ref.1, f32[8,64,128]{2,1,0:T(8,128)} %meas_ref.1, f32[128,64]{1,0:T(8,128)} %bitcast.4, s32[1,64]{1,0:T(1,128)} %bitcast.5), custom_call_target="tpu_custom_call" | custom-call | tf_op jit(solution)/shard_map/pack/pallas_call | solution.py:317
  2.1 35.9 %all_to_all.10.in_ref = f32[16,136,128]{2,1,0:T(8,128)S(1)} all-to-all(f32[16,136,128]{2,1,0:T(8,128)S(1)} %pack.1), channel_id=1, replica_groups=mesh['gx'=8,'gy'=2,'gz'=2] {'gx','gy'}, dimensions={0} | all-to-all | bytes 2228224 | tf_op jit(solution)/shard_map/all_to_all | solution.py:323
  37.9 6.9 %both_ways.1 = f32[16,104,128]{2,1,0:T(8,128)S(1)} custom-call(f32[16,136,128]{2,1,0:T(8,128)S(1)} %all_to_all.10.in_ref), custom_call_target="tpu_custom_call" | custom-call | tf_op jit(solution)/shard_map/both_ways/pallas_call | solution.py:325
  44.8 25.1 %all_to_all.11.in_ref = f32[16,104,128]{2,1,0:T(8,128)S(1)} all-to-all(f32[16,104,128]{2,1,0:T(8,128)S(1)} %both_ways.1), channel_id=1, replica_groups=mesh['gx'=8,'gy'=2,'gz'=2] {'gx','gy'}, dimensions={0} | all-to-all | bytes 1703936 | tf_op jit(solution)/shard_map/all_to_all | solution.py:331
  69.9 0.6 slice_reduce_fusion
  70.5 1.5 %collective-permute-start = (f32[]{:T(128)}, f32[]{:T(128)}, u32[]{:S(2)}, u32[]{:S(2)}) collective-permute-start(f32[]{:T(128)} %slice_reduce_fusion), channel_id=1, source_target_pairs={{0,1},{1,0},{2,3},{3,2},{4,5},{5,4},{6,7},{7,6},{8,9},{9,8},{10,11... | collective-permute-start | bytes 20 | tf_op jit(solution)/shard_map/ppermute | solution.py:215
  72.0 1.1 %unpack.1 = (f32[16,64,128]{2,1,0:T(8,128)}, f32[8,64,128]{2,1,0:T(8,128)}) custom-call(f32[16,104,128]{2,1,0:T(8,128)S(1)} %all_to_all.11.in_ref), custom_call_target="tpu_custom_call" | custom-call | flops 16777216 | bytes 2097152 | tf_op jit(solution)/shard_map/unpack/pallas_call | solution.py:333
  73.1 1.1 %collective-permute-done = f32[]{:T(128)} collective-permute-done((f32[]{:T(128)}, f32[]{:T(128)}, u32[]{:S(2)}, u32[]{:S(2)}) %collective-permute-start) | collective-permute-done | bytes 36 | tf_op jit(solution)/shard_map/ppermute | solution.py:215
Async XLA Ops:
  70.5 3.7 %collective-permute-start = (f32[]{:T(128)}, f32[]{:T(128)}, u32[]{:S(2)}, u32[]{:S(2)}) collective-permute-start(f32[]{:T(128)} %slice_reduce_fusion), channel_id=1, source_target_pairs={{0,1},{1,0},{2,3},{3,2},{4,5},{5,4},{6,7},{7,6},{8,9},{9,8},{10,11... | collective-permute-start | bytes 20 | tf_op jit(solution)/shard_map/ppermute | solution.py:215

commit v5 on v4

--- a/solution.py
+++ b/solution.py
@@ -7,8 +7,10 @@
 from jax.experimental.pallas import tpu as pltpu
 from jax.sharding import PartitionSpec as P
 
+
 LANES = 128
 SUBS = 8
+LIMIT = pltpu.CompilerParams(vmem_limit_bytes=8 << 20)
 STRIDE = 72
 TOGETHER = 2
 
@@ -32,10 +34,16 @@
     return jnp.where(left, first, swap(second)), jnp.where(left, swap(first), second)
 
 
-def pack_kernel(half_rows, vol_ref, meas_ref, w_ref, off_ref, out_ref, flat_ref):
-    cols, rows, depth = vol_ref.shape
+def share_kernel(w_ref, off_ref, out_ref):
+    angles = w_ref.shape[1]
+    out_ref[:angles, :] = w_ref[...].T
+    shift = jnp.concatenate([off_ref[...], jnp.zeros((1, LANES - angles), jnp.int32)], axis=1).astype(jnp.float32)
+    out_ref[angles:, :] = jnp.broadcast_to(shift, (SUBS, LANES))
+
+
+def pack_kernel(vol_ref, meas_ref, out_ref):
+    cols, _, depth = vol_ref.shape
     share = meas_ref.shape[0]
-    wide, angles = w_ref.shape
     peers = out_ref.shape[0]
     deep = depth // peers
     at = 0
@@ -44,13 +52,30 @@
             pair = jnp.concatenate([ref[j], ref[j + count]], axis=0)
             out_ref[:, at : at + deep, :] = pair.T.reshape(peers, deep, LANES)
             at += deep
-    flat_ref[...] = w_ref[...].T
-    start = pl.multiple_of(lax.axis_index("gy") * half_rows, SUBS)
-    part = flat_ref[pl.ds(start, half_rows), :]
-    out_ref[:, at : at + half_rows, :] = jnp.broadcast_to(part, (peers, half_rows, LANES))
-    at += half_rows
-    shift = jnp.concatenate([off_ref[...], jnp.zeros((1, LANES - angles), jnp.int32)], axis=1).astype(jnp.float32)
-    out_ref[:, at : at + SUBS, :] = jnp.broadcast_to(shift, (peers, SUBS, LANES))
+
+
+def prepare_kernel(in_ref, wf_ref, wb_ref, sh_ref):
+    rows, wide = in_ref.shape[-2:]
+    bricks = sh_ref.shape[0] // 2
+    angles = rows - SUBS
+    mine = lax.axis_index("gx")
+    plane = lax.axis_index("gy") * 2 + lax.axis_index("gz")
+    for c in range(2):
+        for y in range(2):
+            for x in range(2):
+                i = mine ^ c ^ (2 * (plane ^ (2 * y + x)))
+                w = in_ref[c, y, x, :angles, :]
+                high, low = split(w)
+                wf_ref[i, :, :wide] = high
+                wf_ref[i, :, wide : 2 * wide] = high
+                wf_ref[i, :, 2 * wide :] = low
+                high, low = split(w.T)
+                wb_ref[i, :, :angles] = high
+                wb_ref[i, :, angles : 2 * angles] = high
+                wb_ref[i, :, 2 * angles :] = low
+                row = in_ref[c, y, x, angles : angles + 1, :].astype(jnp.int32)
+                sh_ref[pl.ds(i, 1), :] = row
+                sh_ref[pl.ds(bricks + i, 1), :] = LANES - row
 
 
 def three(x):
@@ -58,38 +83,20 @@
     return jnp.concatenate([high, low, high], axis=0)
 
 
-def main_kernel(dims, in_ref, out_ref, *scratch):
-    wf_ref, wb_ref, int_ref, sh_ref, total_ref = scratch[:5]
-    turn_refs, sh_sem = scratch[5 : 5 + TOGETHER], scratch[5 + TOGETHER]
+def main_kernel(dims, in_ref, wf_ref, wb_ref, int_ref, out_ref, *scratch):
+    sh_ref, total_ref = scratch[:2]
+    turn_refs, sh_sem = scratch[2 : 2 + TOGETHER], scratch[2 + TOGETHER]
     bricks, groups, cols, taps, angles, share, deep = dims
-    wide = taps * cols
-    piece = angles // groups
     half, quarter = cols // 2, share // 2
     m_at = half * deep
     w_at = m_at + quarter * deep
-    s_at = w_at + piece
-
-    for i in range(bricks):
-        row = in_ref[i * groups, s_at : s_at + 1, :].astype(jnp.int32)
-        int_ref[i : i + 1, :] = row
-        int_ref[bricks + i : bricks + i + 1, :] = LANES - row
+
     to_scalars = pltpu.make_async_copy(int_ref, sh_ref, sh_sem)
     to_scalars.start()
     total_ref[...] = jnp.zeros_like(total_ref)
     lane_c = lane_ids(cols)
     lane = lane_ids(deep)
     zero = jnp.zeros((cols, LANES), jnp.bfloat16)
-
-    def weights_of(i):
-        w = jnp.concatenate([in_ref[i * groups + h, w_at : w_at + piece, :] for h in range(groups)], axis=0)
-        high, low = split(w)
-        wf_ref[i, :, :wide] = high
-        wf_ref[i, :, wide : 2 * wide] = high
-        wf_ref[i, :, 2 * wide :] = low
-        high, low = split(w.T)
-        wb_ref[i, :, :angles] = high
-        wb_ref[i, :, angles : 2 * angles] = high
-        wb_ref[i, :, 2 * angles :] = low
 
     def project(i, turn_ref):
         for q in range(deep // 2):
@@ -122,7 +129,6 @@
     def forward(n, carry):
         i = n * TOGETHER
         for k, turn_ref in enumerate(turn_refs):
-            weights_of(i + k)
             project(i + k, turn_ref)
 
         @pl.when(n == 0)
@@ -176,13 +182,9 @@
 
 
 def main_scratch(dims):
-    bricks, groups, cols, taps, angles, share, deep = dims
-    wide = taps * cols
-    f32, bf16 = jnp.float32, jnp.bfloat16
+    bricks, _, _, _, angles, _, deep = dims
+    f32 = jnp.float32
     return [
-        pltpu.VMEM((bricks, angles, 3 * wide), bf16),
-        pltpu.VMEM((bricks, wide, 3 * angles), bf16),
-        pltpu.VMEM((2 * bricks, LANES), jnp.int32),
         pltpu.SMEM((2 * bricks, LANES), jnp.int32),
         pltpu.VMEM((angles, deep, LANES), f32),
         *[pltpu.VMEM((deep * STRIDE, LANES), f32) for _ in range(TOGETHER)],
@@ -204,8 +206,23 @@
             at += deep
 
 
+def cost(flops):
+    return pl.CostEstimate(flops=flops, bytes_accessed=1 << 21, transcendentals=0)
+
+
+def off_chip(x):
+    return pltpu.with_memory_space_constraint(x, pltpu.HBM)
+
+
 def on_chip(x):
     return pltpu.with_memory_space_constraint(x, pltpu.VMEM)
+
+
+def over_planes(x):
+    sizes = [lax.axis_size(axis) for axis in ("gx", "gy", "gz")]
+    planes = sizes[1] * sizes[2]
+    pairs = [(at * planes + q, (at ^ (2 * q)) * planes + q) for at in range(sizes[0]) for q in range(planes)]
+    return lax.ppermute(x, ("gx", "gy", "gz"), pairs)
 
 
 def butterfly(x, axis):
@@ -274,7 +291,7 @@
         grad = grad + jnp.einsum("adc,adyz->cyz", wb, sheared, precision=lax.Precision.HIGHEST)
         return (grad, None)
 
-    gradient, unused = lax.scan(
+    gradient, _ = lax.scan(
         backward, jnp.zeros((cols, rows, depth), jnp.float32), (wblk, sblk, rblk)
     )
     entries = angles * rows * depth * lax.axis_size("gy") * lax.axis_size("gz")
@@ -289,6 +306,8 @@
     deep, rest = divmod(depth, lax.axis_size("gx") * groups)
     return (
         groups == 2
+        and lax.axis_size("gz") == 2
+        and lax.axis_size("gx") == 8
         and 2 * rows == LANES
         and depth == LANES
         and rest == 0
@@ -310,31 +329,46 @@
     groups = lax.axis_size("gy")
     peers = bricks * groups
     deep = depth // peers
-    piece = angles // groups
     moved = (cols // 2 + share // 2) * deep
-    sent = moved + piece + SUBS
     f32 = jnp.float32
+    wide = taps * cols
+    part = pl.pallas_call(
+        share_kernel,
+        out_shape=pltpu.VMEM((angles + SUBS, wide), f32),
+        compiler_params=LIMIT, name="share",
+    )(off_chip(weights.transpose(1, 2, 0).reshape(wide, angles)), off_chip(offsets.reshape(1, angles)))
+    part = over_planes(part)
     payload = pl.pallas_call(
-        functools.partial(pack_kernel, piece),
-        out_shape=pltpu.VMEM((peers, sent, LANES), f32),
-        scratch_shapes=[pltpu.VMEM((angles, LANES), f32)],
-        name="pack",
-    )(volume, measured, weights.transpose(1, 2, 0).reshape(taps * cols, angles), offsets.reshape(1, angles))
+        pack_kernel, out_shape=pltpu.VMEM((peers, moved, LANES), f32), cost_estimate=cost(1 << 24), compiler_params=LIMIT, name="pack"
+    )(off_chip(volume), off_chip(measured))
     arrived = lax.all_to_all(payload, ("gx", "gy"), 0, 0, tiled=True)
+    for axis in ("gz", "gy", "gx"):
+        pairs = [(i, i ^ 1) for i in range(lax.axis_size(axis))]
+        part = jnp.stack([part, lax.ppermute(part, axis, pairs)])
+    prepared = pl.pallas_call(
+        prepare_kernel,
+        out_shape=(
+            pltpu.VMEM((bricks, angles, 3 * wide), jnp.bfloat16),
+            pltpu.VMEM((bricks, wide, 3 * angles), jnp.bfloat16),
+            pltpu.VMEM((2 * bricks, LANES), jnp.int32),
+        ),
+        cost_estimate=cost(1 << 26),
+        compiler_params=LIMIT, name="prepare",
+    )(on_chip(part))
     dims = (bricks, groups, cols, taps, angles, share, deep)
     payload = pl.pallas_call(
         functools.partial(main_kernel, dims),
         out_shape=pltpu.VMEM((peers, moved + SUBS, LANES), f32),
         scratch_shapes=main_scratch(dims),
-        name="both_ways",
-    )(on_chip(arrived))
+        compiler_params=LIMIT, name="both_ways",
+    )(on_chip(arrived), *map(on_chip, prepared))
     arrived = lax.all_to_all(payload, ("gx", "gy"), 0, 0, tiled=True)
     square = butterfly(jnp.sum(arrived[:, moved:]), "gz")
     gradient, resid = pl.pallas_call(
         unpack_kernel,
         out_shape=(jax.ShapeDtypeStruct(volume.shape, f32), jax.ShapeDtypeStruct(measured.shape, f32)),
-        cost_estimate=pl.CostEstimate(flops=1 << 24, bytes_accessed=1 << 21, transcendentals=0),
-        name="unpack",
+        cost_estimate=cost(1 << 24),
+        compiler_params=LIMIT, name="unpack",
     )(on_chip(arrived))
     entries = angles * rows * depth * groups * lax.axis_size("gz")
     misfit = square / entries

time: 76.9 us -> 82.8 us (1.077)
  blocking collectives: 61 us -> 26.5 us
  starting transfers between devices: 1.49 us -> 33.2 us
  waiting for transfers between devices: 1.09 us -> 7.56 us
  Pallas kernels: 9.36 us -> 11.4 us
    all_to_all x2 -> x1, blocking collectives: 61 us -> 26.5 us  [body(): arrived = lax.all_to_all(payload, ('gx', 'gy'), 0, 0, tiled=True)]
    ppermute x0 -> x4, starting transfers between devices: none -> 25.2 us  [the longest x3 24.5 us: body(): part = jnp.stack([part, lax.ppermute(part, axis, pairs)])]
    all_to_all x0 -> x1, starting transfers between devices: none -> 7.41 us  [body(): arrived = lax.all_to_all(payload, ('gx', 'gy'), 0, 0, tiled=True)]
    ppermute x0 -> x4, waiting for transfers between devices: none -> 5.63 us  [the longest x3 5.63 us: body(): part = jnp.stack([part, lax.ppermute(part, axis, pairs)])]
    pallas_call x1 -> x3, Pallas kernels: 1.43 us -> 3.57 us  [the longest x1 2.26 us: body(): pl.pallas_call(pack_kernel, out_shape=pltpu.VMEM((peers, moved, LANES), f...]
    ppermute x1, starting transfers between devices: 1.49 us -> 0.65 us  [butterfly(): x = x + lax.ppermute(x, axis, [(i, i ^ step) for i in range(count)])]
    ppermute x1, waiting for transfers between devices: 1.09 us -> 1.93 us  [butterfly(): x = x + lax.ppermute(x, axis, [(i, i ^ step) for i in range(count)])]
  transfers between devices with their start and end apart: 1 -> 6, of which waited for: 1 -> 4; matrix products, arithmetic and copies ran while one was open for 0% -> 0% of each run, Pallas kernels for 1% -> 3%
where the time goes in v5:
time: 82.8 us; the launch traced here: 82.5 us
  starting transfers between devices  33.2 us (40%)
  blocking collectives  26.5 us (32%)
  Pallas kernels  11.4 us (14%)
  waiting for transfers between devices  7.56 us (9%)
  between operations  3.16 us (4%)
    all_to_all x1, blocking collectives, body(): arrived = lax.all_to_all(payload, ('gx', 'gy'), 0, 0, tiled=True)  26.5 us
    ppermute x3, starting transfers between devices, body(): part = jnp.stack([part, lax.ppermute(part, axis, pairs)])  24.5 us
    all_to_all x1, starting transfers between devices, body(): arrived = lax.all_to_all(payload, ('gx', 'gy'), 0, 0, tiled=True)  7.41 us
    pallas_call x1, Pallas kernels, body(): pl.pallas_call(functools.partial(main_kernel, dims), out_shape=pltpu.VMEM...  6.77 us
    ppermute x3, waiting for transfers between devices, body(): part = jnp.stack([part, lax.ppermute(part, axis, pairs)])  5.63 us
    pallas_call x1, Pallas kernels, body(): pl.pallas_call(pack_kernel, out_shape=pltpu.VMEM((peers, moved, LANES), f...  2.26 us
    ppermute x1, waiting for transfers between devices, butterfly(): x = x + lax.ppermute(x, axis, [(i, i ^ step) for i in range(count)])  1.93 us
  transfers between devices with their start and end apart: 6, of which 4 were waited for; matrix products, arithmetic and copies ran while one was open for 0% of the time, Pallas kernels for 3%

profile of v5, /device:TPU:0, one launch (start us, length us, event | category | flops | bytes accessed | tf_op | source)
XLA Modules:
  0.0 82.5 jit_solution(17927164880416799332)
XLA Ops:
  0.6 2.3 %pack.1 = f32[16,96,128]{2,1,0:T(8,128)} custom-call(f32[16,64,128]{2,1,0:T(8,128)} %vol_ref.1, f32[8,64,128]{2,1,0:T(8,128)} %meas_ref.1), custom_call_target="tpu_custom_call" | custom-call | flops 16777216 | bytes 2097152 | tf_op jit(solution)/shard_map/pack/pallas_call | solution.py:341
  2.9 7.4 %all-to-all-start = ((f32[16,96,128]{2,1,0:T(8,128)}), f32[16,96,128]{2,1,0:T(8,128)S(1)}, u32[]{:S(2)}, u32[]{:S(2)}) async-start(f32[16,96,128]{2,1,0:T(8,128)} %pack.1), calls=%async_computation | async-start | bytes 1572864 | tf_op jit(solution)/shard_map/all_to_all | solution.py:344
  10.3 0.9 %share.1 = f32[72,128]{1,0:T(8,128)S(1)} custom-call(f32[128,64]{1,0:T(8,128)} %bitcast.14, s32[1,64]{1,0:T(1,128)} %bitcast.17), custom_call_target="tpu_custom_call" | custom-call | tf_op jit(solution)/shard_map/share/pallas_call | solution.py:335
  11.2 0.7 collective-permute-start
  11.9 0.0 collective-permute-done
  11.9 14.4 %collective-permute-start.1 = (f32[72,128]{1,0:T(8,128)S(1)}, f32[72,128]{1,0:T(8,128)S(1)}, u32[]{:S(2)}, u32[]{:S(2)}) collective-permute-start(f32[72,128]{1,0:T(8,128)S(1)} %collective-permute-done), channel_id=1, source_target_pairs={{0,1},{1,0},{2,3},{3,2},{4,5},{5,4},{6,7},{7,6},{8,9},{9,8},{10,11... | collective-permute-start | bytes 110600 | tf_op jit(solution)/shard_map/ppermute | solution.py:347
  26.3 1.9 %collective-permute-done.1 = f32[72,128]{1,0:T(8,128)S(1)} collective-permute-done((f32[72,128]{1,0:T(8,128)S(1)}, f32[72,128]{1,0:T(8,128)S(1)}, u32[]{:S(2)}, u32[]{:S(2)}) %collective-permute-start.1) | collective-permute-done | bytes 36896 | tf_op jit(solution)/shard_map/ppermute | solution.py:347
  28.3 10.0 %collective-permute-start.2 = (f32[2,72,128]{2,1,0:T(8,128)S(1)}, f32[2,72,128]{2,1,0:T(8,128)S(1)}, u32[]{:S(2)}, u32[]{:S(2)}) collective-permute-start(f32[2,72,128]{2,1,0:T(8,128)S(1)} %get-tuple-element.16), channel_id=1, source_target_pairs={{0,2},{2,0},{1,3},{3,1},{4,6},{6,4},{5,7},{7,5},{8,10},{10,8},{9,1... | collective-permute-start | bytes 221192 | tf_op jit(solution)/shard_map/ppermute | solution.py:347
  38.3 2.3 %collective-permute-done.2 = f32[2,72,128]{2,1,0:T(8,128)S(1)} collective-permute-done((f32[2,72,128]{2,1,0:T(8,128)S(1)}, f32[2,72,128]{2,1,0:T(8,128)S(1)}, u32[]{:S(2)}, u32[]{:S(2)}) %collective-permute-start.2) | collective-permute-done | bytes 73760 | tf_op jit(solution)/shard_map/ppermute | solution.py:347
  40.7 0.1 collective-permute-start.3
  40.7 1.4 %collective-permute-done.3 = f32[2,2,72,128]{3,2,1,0:T(8,128)S(1)} collective-permute-done((f32[2,2,72,128]{3,2,1,0:T(8,128)S(1)}, f32[2,2,72,128]{3,2,1,0:T(8,128)S(1)}, u32[]{:S(2)}, u32[]{:S(2)}) %collective-permute-start.3) | collective-permute-done | bytes 147488 | tf_op jit(solution)/shard_map/ppermute | solution.py:347
  42.1 0.4 prepare.1
  42.5 0.0 all-to-all-done.in_ref
  42.5 6.8 %both_ways.1 = f32[16,104,128]{2,1,0:T(8,128)S(1)} custom-call(f32[16,96,128]{2,1,0:T(8,128)S(1)} %all-to-all-done.in_ref, bf16[8,64,384]{2,1,0:T(8,128)(2,1)S(1)} %get-tuple-element.8.wf_ref, bf16[8,128,192]{2,1,0:T(8,128)(2,1)S(1)} %get-tuple-element.9.wb_ref, s32[16,128]{1,0:T(8,128)S(1)} %get-tuple-element.10.int_ref), custom_call_target="tpu_custom_call" | custom-call | tf_op jit(solution)/shard_map/both_ways/pallas_call | solution.py:359
  49.3 26.5 %all_to_all.10.in_ref = f32[16,104,128]{2,1,0:T(8,128)S(1)} all-to-all(f32[16,104,128]{2,1,0:T(8,128)S(1)} %both_ways.1), channel_id=1, replica_groups=mesh['gx'=8,'gy'=2,'gz'=2] {'gx','gy'}, dimensions={0} | all-to-all | bytes 1703936 | tf_op jit(solution)/shard_map/all_to_all | solution.py:365
  75.8 0.6 slice_reduce_fusion
  76.4 0.6 collective-permute-start.4
  77.0 1.1 %unpack.1 = (f32[16,64,128]{2,1,0:T(8,128)}, f32[8,64,128]{2,1,0:T(8,128)}) custom-call(f32[16,104,128]{2,1,0:T(8,128)S(1)} %all_to_all.10.in_ref), custom_call_target="tpu_custom_call" | custom-call | flops 16777216 | bytes 2097152 | tf_op jit(solution)/shard_map/unpack/pallas_call | solution.py:367
  78.1 1.9 %collective-permute-done.4 = f32[]{:T(128)} collective-permute-done((f32[]{:T(128)}, f32[]{:T(128)}, u32[]{:S(2)}, u32[]{:S(2)}) %collective-permute-start.4) | collective-permute-done | bytes 36 | tf_op jit(solution)/shard_map/ppermute | solution.py:232
  (3 shorter events, 0.1 us)
Async XLA Ops:
  2.9 39.6 %all-to-all-start = ((f32[16,96,128]{2,1,0:T(8,128)}), f32[16,96,128]{2,1,0:T(8,128)S(1)}, u32[]{:S(2)}, u32[]{:S(2)}) async-start(f32[16,96,128]{2,1,0:T(8,128)} %pack.1), calls=%async_computation | async-start | bytes 1572864 | tf_op jit(solution)/shard_map/all_to_all | solution.py:344
  11.2 0.7 collective-permute-start
  11.9 16.4 %collective-permute-start.1 = (f32[72,128]{1,0:T(8,128)S(1)}, f32[72,128]{1,0:T(8,128)S(1)}, u32[]{:S(2)}, u32[]{:S(2)}) collective-permute-start(f32[72,128]{1,0:T(8,128)S(1)} %collective-permute-done), channel_id=1, source_target_pairs={{0,1},{1,0},{2,3},{3,2},{4,5},{5,4},{6,7},{7,6},{8,9},{9,8},{10,11... | collective-permute-start | bytes 110600 | tf_op jit(solution)/shard_map/ppermute | solution.py:347
  28.3 12.3 %collective-permute-start.2 = (f32[2,72,128]{2,1,0:T(8,128)S(1)}, f32[2,72,128]{2,1,0:T(8,128)S(1)}, u32[]{:S(2)}, u32[]{:S(2)}) collective-permute-start(f32[2,72,128]{2,1,0:T(8,128)S(1)} %get-tuple-element.16), channel_id=1, source_target_pairs={{0,2},{2,0},{1,3},{3,1},{4,6},{6,4},{5,7},{7,5},{8,10},{10,8},{9,1... | collective-permute-start | bytes 221192 | tf_op jit(solution)/shard_map/ppermute | solution.py:347
  40.7 1.4 %collective-permute-start.3 = (f32[2,2,72,128]{3,2,1,0:T(8,128)S(1)}, f32[2,2,72,128]{3,2,1,0:T(8,128)S(1)}, u32[]{:S(2)}, u32[]{:S(2)}) collective-permute-start(f32[2,2,72,128]{3,2,1,0:T(8,128)S(1)} %get-tuple-element.14), channel_id=1, source_target_pairs={{0,4},{4,0},{8,12},{12,8},{16,20},{20,16},{24,28},{28,24},{1,5},{5... | collective-permute-start | bytes 442376 | tf_op jit(solution)/shard_map/ppermute | solution.py:347
  76.4 3.7 %collective-permute-start.4 = (f32[]{:T(128)}, f32[]{:T(128)}, u32[]{:S(2)}, u32[]{:S(2)}) collective-permute-start(f32[]{:T(128)} %slice_reduce_fusion), channel_id=1, source_target_pairs={{0,1},{1,0},{2,3},{3,2},{4,5},{5,4},{6,7},{7,6},{8,9},{9,8},{10,11... | collective-permute-start | bytes 20 | tf_op jit(solution)/shard_map/ppermute | solution.py:232

commit v6 on v5

--- a/solution.py
+++ b/solution.py
@@ -29,27 +29,31 @@
     return pltpu.roll(x, LANES // 2, 1)
 
 
-def unpair(first, second):
+def parted(first, second):
     left = lane_ids(first.shape[0]) < LANES // 2
-    return jnp.where(left, first, swap(second)), jnp.where(left, swap(first), second)
-
-
-def share_kernel(w_ref, off_ref, out_ref):
-    angles = w_ref.shape[1]
-    out_ref[:angles, :] = w_ref[...].T
-    shift = jnp.concatenate([off_ref[...], jnp.zeros((1, LANES - angles), jnp.int32)], axis=1).astype(jnp.float32)
-    out_ref[angles:, :] = jnp.broadcast_to(shift, (SUBS, LANES))
-
-
-def pack_kernel(vol_ref, meas_ref, out_ref):
+    return jnp.where(left, first, second), swap(jnp.where(left, second, first))
+
+
+def joined(low, high):
+    left = lane_ids(low.shape[0]) < LANES // 2
+    high = swap(high)
+    return jnp.where(left, low, high), jnp.where(left, high, low)
+
+
+def pack_kernel(vol_ref, meas_ref, w_ref, off_ref, out_ref, part_ref):
     cols, _, depth = vol_ref.shape
     share = meas_ref.shape[0]
+    angles = w_ref.shape[1]
     peers = out_ref.shape[0]
     deep = depth // peers
+    second = lax.axis_index("gy")
+    part_ref[:angles, :] = w_ref[...].T
+    shift = jnp.concatenate([off_ref[...], jnp.zeros((1, LANES - angles), jnp.int32)], axis=1).astype(jnp.float32)
+    part_ref[angles:, :] = jnp.broadcast_to(shift, (SUBS, LANES))
     at = 0
     for ref, count in ((vol_ref, cols // 2), (meas_ref, share // 2)):
         for j in range(count):
-            pair = jnp.concatenate([ref[j], ref[j + count]], axis=0)
+            pair = jnp.concatenate([ref[j + second * count], ref[j + (1 - second) * count]], axis=0)
             out_ref[:, at : at + deep, :] = pair.T.reshape(peers, deep, LANES)
             at += deep
 
@@ -66,9 +70,10 @@
                 i = mine ^ c ^ (2 * (plane ^ (2 * y + x)))
                 w = in_ref[c, y, x, :angles, :]
                 high, low = split(w)
-                wf_ref[i, :, :wide] = high
-                wf_ref[i, :, wide : 2 * wide] = high
-                wf_ref[i, :, 2 * wide :] = low
+                wf_ref[i, :angles, :wide] = high
+                wf_ref[i, :angles, wide:] = high
+                wf_ref[i, angles:, :wide] = low
+                wf_ref[i, angles:, wide:] = jnp.zeros_like(low)
                 high, low = split(w.T)
                 wb_ref[i, :, :angles] = high
                 wb_ref[i, :, angles : 2 * angles] = high
@@ -103,16 +108,16 @@
             blocks = []
             for z in (2 * q, 2 * q + 1):
                 first, second = (in_ref[i * groups + h, pl.ds(z, half, stride=deep), :] for h in range(2))
-                x = jnp.concatenate(unpair(first, second), axis=0)
+                x = jnp.concatenate(parted(first, second), axis=0)
                 parts = []
                 for part in split(x):
                     moved = [part]
                     for tap in range(1, taps):
                         moved.append(jnp.where(lane_c < LANES - tap, pltpu.roll(part, LANES - tap, 1), zero))
                     parts.append(jnp.concatenate(moved, axis=0))
-                high, low = parts
-                blocks.append(jnp.concatenate([high, low, high], axis=0))
+                blocks.append(jnp.concatenate(parts, axis=0))
             out = jnp.dot(wf_ref[i], jnp.concatenate(blocks, axis=1), preferred_element_type=jnp.float32)
+            out = out[:angles] + out[angles:]
             for k in range(2):
                 at = (2 * q + k) * STRIDE
                 turn_ref[at : at + angles, :] = out[:, k * LANES : (k + 1) * LANES]
@@ -153,7 +158,7 @@
                 total = part[:cols]
                 for tap in range(1, taps):
                     total = total + jnp.where(lane_c >= tap, pltpu.roll(part[tap * cols : (tap + 1) * cols], tap, 1), 0.0)
-                for h, block in enumerate(unpair(total[:half], total[half:])):
+                for h, block in enumerate(joined(total[:half], total[half:])):
                     out_ref[i * groups + h, pl.ds(z, half, stride=deep), :] = block
 
     def backward(n, carry):
@@ -170,11 +175,11 @@
         for j in range(quarter):
             at = m_at + j * deep
             low_at, high_at = i * share + j, i * share + quarter + j
-            low, high = unpair(*(in_ref[i * groups + h, at : at + deep, :] for h in range(2)))
+            low, high = parted(*(in_ref[i * groups + h, at : at + deep, :] for h in range(2)))
             low, high = total_ref[low_at] - low, total_ref[high_at] - high
             total_ref[low_at], total_ref[high_at] = low, high
             square = square + low * low + high * high
-            for h, block in enumerate(unpair(low, high)):
+            for h, block in enumerate(joined(low, high)):
                 out_ref[i * groups + h, at : at + deep, :] = block
     for p in range(bricks * groups):
         out_ref[p, w_at : w_at + deep, :] = square
@@ -197,12 +202,13 @@
     cols, rows, depth = grad_ref.shape
     share = res_ref.shape[0]
     deep = depth // peers
+    second = lax.axis_index("gy")
     at = 0
     for ref, count in ((grad_ref, cols // 2), (res_ref, share // 2)):
         for j in range(count):
             both = in_ref[:, at : at + deep, :].reshape(depth, LANES).T
-            ref[j] = both[:rows]
-            ref[j + count] = both[rows:]
+            ref[j + second * count] = both[:rows]
+            ref[j + (1 - second) * count] = both[rows:]
             at += deep
 
 
@@ -332,15 +338,18 @@
     moved = (cols // 2 + share // 2) * deep
     f32 = jnp.float32
     wide = taps * cols
-    part = pl.pallas_call(
-        share_kernel,
-        out_shape=pltpu.VMEM((angles + SUBS, wide), f32),
-        compiler_params=LIMIT, name="share",
-    )(off_chip(weights.transpose(1, 2, 0).reshape(wide, angles)), off_chip(offsets.reshape(1, angles)))
+    payload, part = pl.pallas_call(
+        pack_kernel,
+        out_shape=(pltpu.VMEM((peers, moved, LANES), f32), pltpu.VMEM((angles + SUBS, wide), f32)),
+        compiler_params=LIMIT,
+        name="pack",
+    )(
+        off_chip(volume),
+        off_chip(measured),
+        off_chip(weights.transpose(1, 2, 0).reshape(wide, angles)),
+        off_chip(offsets.reshape(1, angles)),
+    )
     part = over_planes(part)
-    payload = pl.pallas_call(
-        pack_kernel, out_shape=pltpu.VMEM((peers, moved, LANES), f32), cost_estimate=cost(1 << 24), compiler_params=LIMIT, name="pack"
-    )(off_chip(volume), off_chip(measured))
     arrived = lax.all_to_all(payload, ("gx", "gy"), 0, 0, tiled=True)
     for axis in ("gz", "gy", "gx"):
         pairs = [(i, i ^ 1) for i in range(lax.axis_size(axis))]
@@ -348,7 +357,7 @@
     prepared = pl.pallas_call(
         prepare_kernel,
         out_shape=(
-            pltpu.VMEM((bricks, angles, 3 * wide), jnp.bfloat16),
+            pltpu.VMEM((bricks, 2 * angles, 2 * wide), jnp.bfloat16),
             pltpu.VMEM((bricks, wide, 3 * angles), jnp.bfloat16),
             pltpu.VMEM((2 * bricks, LANES), jnp.int32),
         ),

time: 82.8 us -> 82.2 us (level)
  Pallas kernels: 11.4 us -> 10 us
  starting transfers between devices: 33.2 us -> 34.1 us
    ppermute x3, starting transfers between devices: 24.5 us -> 25.4 us  [body(): part = jnp.stack([part, lax.ppermute(part, axis, pairs)])]
    pallas_call x3 -> x2, Pallas kernels: 3.57 us -> 2.72 us  [the longest x1 2.31 us: body(): pl.pallas_call(pack_kernel, out_shape=(pltpu.VMEM((peers, moved, LANES),...]
  transfers between devices with their start and end apart: 6 -> 6, of which waited for: 4 -> 4; matrix products, arithmetic and copies ran while one was open for 0% -> 0% of each run, Pallas kernels for 3% -> 2%
where the time goes in v6:
time: 82.2 us; the launch traced here: 81.9 us
  starting transfers between devices  34.1 us (41%)
  blocking collectives  26.5 us (32%)
  Pallas kernels  10 us (12%)
  waiting for transfers between devices  7.57 us (9%)
  between operations  3.1 us (4%)
    all_to_all x1, blocking collectives, body(): arrived = lax.all_to_all(payload, ('gx', 'gy'), 0, 0, tiled=True)  26.5 us
    ppermute x3, starting transfers between devices, body(): part = jnp.stack([part, lax.ppermute(part, axis, pairs)])  25.4 us
    all_to_all x1, starting transfers between devices, body(): arrived = lax.all_to_all(payload, ('gx', 'gy'), 0, 0, tiled=True)  7.41 us
    pallas_call x1, Pallas kernels, body(): pl.pallas_call(functools.partial(main_kernel, dims), out_shape=pltpu.VMEM...  6.21 us
    ppermute x3, waiting for transfers between devices, body(): part = jnp.stack([part, lax.ppermute(part, axis, pairs)])  5.63 us
    pallas_call x1, Pallas kernels, body(): pl.pallas_call(pack_kernel, out_shape=(pltpu.VMEM((peers, moved, LANES),...  2.31 us
    ppermute x1, waiting for transfers between devices, butterfly(): x = x + lax.ppermute(x, axis, [(i, i ^ step) for i in range(count)])  1.94 us
  transfers between devices with their start and end apart: 6, of which 4 were waited for; matrix products, arithmetic and copies ran while one was open for 0% of the time, Pallas kernels for 2%

profile of v6, /device:TPU:0, one launch (start us, length us, event | category | flops | bytes accessed | tf_op | source)
XLA Modules:
  0.0 81.9 jit_solution(1457155965415402932)
XLA Ops:
  0.6 2.3 %pack.1 = (f32[16,96,128]{2,1,0:T(8,128)}, f32[72,128]{1,0:T(8,128)S(1)}) custom-call(f32[16,64,128]{2,1,0:T(8,128)} %vol_ref.1, f32[8,64,128]{2,1,0:T(8,128)} %meas_ref.1, f32[128,64]{1,0:T(8,128)} %bitcast.14, s32[1,64]{1,0:T(1,128)} %bitcast.17), custom_call_target="tpu_custom_call" | custom-call | tf_op jit(solution)/shard_map/pack/pallas_call | solution.py:341
  2.9 7.4 %all-to-all-start = ((f32[16,96,128]{2,1,0:T(8,128)}), f32[16,96,128]{2,1,0:T(8,128)S(1)}, u32[]{:S(2)}, u32[]{:S(2)}) async-start(f32[16,96,128]{2,1,0:T(8,128)} %get-tuple-element.10), calls=%async_computation | async-start | bytes 1572864 | tf_op jit(solution)/shard_map/all_to_all | solution.py:353
  10.4 0.7 collective-permute-start
  11.0 0.0 collective-permute-done
  11.0 15.3 %collective-permute-start.1 = (f32[72,128]{1,0:T(8,128)S(1)}, f32[72,128]{1,0:T(8,128)S(1)}, u32[]{:S(2)}, u32[]{:S(2)}) collective-permute-start(f32[72,128]{1,0:T(8,128)S(1)} %collective-permute-done), channel_id=1, source_target_pairs={{0,1},{1,0},{2,3},{3,2},{4,5},{5,4},{6,7},{7,6},{8,9},{9,8},{10,11... | collective-permute-start | bytes 110600 | tf_op jit(solution)/shard_map/ppermute | solution.py:356
  26.4 1.9 %collective-permute-done.1 = f32[72,128]{1,0:T(8,128)S(1)} collective-permute-done((f32[72,128]{1,0:T(8,128)S(1)}, f32[72,128]{1,0:T(8,128)S(1)}, u32[]{:S(2)}, u32[]{:S(2)}) %collective-permute-start.1) | collective-permute-done | bytes 36896 | tf_op jit(solution)/shard_map/ppermute | solution.py:356
  28.3 10.0 %collective-permute-start.2 = (f32[2,72,128]{2,1,0:T(8,128)S(1)}, f32[2,72,128]{2,1,0:T(8,128)S(1)}, u32[]{:S(2)}, u32[]{:S(2)}) collective-permute-start(f32[2,72,128]{2,1,0:T(8,128)S(1)} %get-tuple-element.20), channel_id=1, source_target_pairs={{0,2},{2,0},{1,3},{3,1},{4,6},{6,4},{5,7},{7,5},{8,10},{10,8},{9,1... | collective-permute-start | bytes 221192 | tf_op jit(solution)/shard_map/ppermute | solution.py:356
  38.3 2.3 %collective-permute-done.2 = f32[2,72,128]{2,1,0:T(8,128)S(1)} collective-permute-done((f32[2,72,128]{2,1,0:T(8,128)S(1)}, f32[2,72,128]{2,1,0:T(8,128)S(1)}, u32[]{:S(2)}, u32[]{:S(2)}) %collective-permute-start.2) | collective-permute-done | bytes 73760 | tf_op jit(solution)/shard_map/ppermute | solution.py:356
  40.7 0.1 collective-permute-start.3
  40.8 1.4 %collective-permute-done.3 = f32[2,2,72,128]{3,2,1,0:T(8,128)S(1)} collective-permute-done((f32[2,2,72,128]{3,2,1,0:T(8,128)S(1)}, f32[2,2,72,128]{3,2,1,0:T(8,128)S(1)}, u32[]{:S(2)}, u32[]{:S(2)}) %collective-permute-start.3) | collective-permute-done | bytes 147488 | tf_op jit(solution)/shard_map/ppermute | solution.py:356
  42.2 0.4 prepare.1
  42.6 0.0 all-to-all-done.in_ref
  42.6 6.2 %both_ways.1 = f32[16,104,128]{2,1,0:T(8,128)S(1)} custom-call(f32[16,96,128]{2,1,0:T(8,128)S(1)} %all-to-all-done.in_ref, bf16[8,128,256]{2,1,0:T(8,128)(2,1)S(1)} %get-tuple-element.12.wf_ref, bf16[8,128,192]{2,1,0:T(8,128)(2,1)S(1)} %get-tuple-element.13.wb_ref, s32[16,128]{1,0:T(8,128)S(1)} %get-tuple-element.14.int_ref), custom_call_target="tpu_custom_call" | custom-call | tf_op jit(solution)/shard_map/both_ways/pallas_call | solution.py:368
  48.8 26.5 %all_to_all.10.in_ref = f32[16,104,128]{2,1,0:T(8,128)S(1)} all-to-all(f32[16,104,128]{2,1,0:T(8,128)S(1)} %both_ways.1), channel_id=1, replica_groups=mesh['gx'=8,'gy'=2,'gz'=2] {'gx','gy'}, dimensions={0} | all-to-all | bytes 1703936 | tf_op jit(solution)/shard_map/all_to_all | solution.py:374
  75.3 0.6 slice_reduce_fusion
  75.9 0.6 collective-permute-start.4
  76.5 1.1 %unpack.1 = (f32[16,64,128]{2,1,0:T(8,128)}, f32[8,64,128]{2,1,0:T(8,128)}) custom-call(f32[16,104,128]{2,1,0:T(8,128)S(1)} %all_to_all.10.in_ref), custom_call_target="tpu_custom_call" | custom-call | flops 16777216 | bytes 2097152 | tf_op jit(solution)/shard_map/unpack/pallas_call | solution.py:376
  77.6 1.9 %collective-permute-done.4 = f32[]{:T(128)} collective-permute-done((f32[]{:T(128)}, f32[]{:T(128)}, u32[]{:S(2)}, u32[]{:S(2)}) %collective-permute-start.4) | collective-permute-done | bytes 36 | tf_op jit(solution)/shard_map/ppermute | solution.py:238
  (3 shorter events, 0.1 us)
Async XLA Ops:
  2.9 39.6 %all-to-all-start = ((f32[16,96,128]{2,1,0:T(8,128)}), f32[16,96,128]{2,1,0:T(8,128)S(1)}, u32[]{:S(2)}, u32[]{:S(2)}) async-start(f32[16,96,128]{2,1,0:T(8,128)} %get-tuple-element.10), calls=%async_computation | async-start | bytes 1572864 | tf_op jit(solution)/shard_map/all_to_all | solution.py:353
  10.4 0.7 collective-permute-start
  11.0 17.3 %collective-permute-start.1 = (f32[72,128]{1,0:T(8,128)S(1)}, f32[72,128]{1,0:T(8,128)S(1)}, u32[]{:S(2)}, u32[]{:S(2)}) collective-permute-start(f32[72,128]{1,0:T(8,128)S(1)} %collective-permute-done), channel_id=1, source_target_pairs={{0,1},{1,0},{2,3},{3,2},{4,5},{5,4},{6,7},{7,6},{8,9},{9,8},{10,11... | collective-permute-start | bytes 110600 | tf_op jit(solution)/shard_map/ppermute | solution.py:356
  28.3 12.3 %collective-permute-start.2 = (f32[2,72,128]{2,1,0:T(8,128)S(1)}, f32[2,72,128]{2,1,0:T(8,128)S(1)}, u32[]{:S(2)}, u32[]{:S(2)}) collective-permute-start(f32[2,72,128]{2,1,0:T(8,128)S(1)} %get-tuple-element.20), channel_id=1, source_target_pairs={{0,2},{2,0},{1,3},{3,1},{4,6},{6,4},{5,7},{7,5},{8,10},{10,8},{9,1... | collective-permute-start | bytes 221192 | tf_op jit(solution)/shard_map/ppermute | solution.py:356
  40.7 1.4 %collective-permute-start.3 = (f32[2,2,72,128]{3,2,1,0:T(8,128)S(1)}, f32[2,2,72,128]{3,2,1,0:T(8,128)S(1)}, u32[]{:S(2)}, u32[]{:S(2)}) collective-permute-start(f32[2,2,72,128]{3,2,1,0:T(8,128)S(1)} %get-tuple-element.18), channel_id=1, source_target_pairs={{0,4},{4,0},{8,12},{12,8},{16,20},{20,16},{24,28},{28,24},{1,5},{5... | collective-permute-start | bytes 442376 | tf_op jit(solution)/shard_map/ppermute | solution.py:356
  75.9 3.7 %collective-permute-start.4 = (f32[]{:T(128)}, f32[]{:T(128)}, u32[]{:S(2)}, u32[]{:S(2)}) collective-permute-start(f32[]{:T(128)} %slice_reduce_fusion), channel_id=1, source_target_pairs={{0,1},{1,0},{2,3},{3,2},{4,5},{5,4},{6,7},{7,6},{8,9},{9,8},{10,11... | collective-permute-start | bytes 20 | tf_op jit(solution)/shard_map/ppermute | solution.py:238

commit v7 on v6

--- a/solution.py
+++ b/solution.py
@@ -12,7 +12,7 @@
 SUBS = 8
 LIMIT = pltpu.CompilerParams(vmem_limit_bytes=8 << 20)
 STRIDE = 72
-TOGETHER = 2
+TOGETHER = 4
 
 
 def split(x):
@@ -162,11 +162,10 @@
                     out_ref[i * groups + h, pl.ds(z, half, stride=deep), :] = block
 
     def backward(n, carry):
-        i = n * TOGETHER
-        for k, turn_ref in enumerate(turn_refs):
-            scatter_rows(i + k, turn_ref)
-        for k, turn_ref in enumerate(turn_refs):
-            backproject(i + k, turn_ref)
+        i = 2 * n
+        for k in range(2):
+            scatter_rows(i + k, turn_refs[k])
+            backproject(i + k, turn_refs[k])
         return carry
 
     lax.fori_loop(0, bricks // TOGETHER, forward, 0)
@@ -183,7 +182,7 @@
                 out_ref[i * groups + h, at : at + deep, :] = block
     for p in range(bricks * groups):
         out_ref[p, w_at : w_at + deep, :] = square
-    lax.fori_loop(0, bricks // TOGETHER, backward, 0)
+    lax.fori_loop(0, bricks // 2, backward, 0)
 
 
 def main_scratch(dims):
@@ -372,15 +371,14 @@
         compiler_params=LIMIT, name="both_ways",
     )(on_chip(arrived), *map(on_chip, prepared))
     arrived = lax.all_to_all(payload, ("gx", "gy"), 0, 0, tiled=True)
-    square = butterfly(jnp.sum(arrived[:, moved:]), "gz")
+    entries = angles * rows * depth * groups * lax.axis_size("gz")
+    misfit = butterfly(jnp.sum(arrived[:, moved:]) / entries, "gz")
     gradient, resid = pl.pallas_call(
         unpack_kernel,
         out_shape=(jax.ShapeDtypeStruct(volume.shape, f32), jax.ShapeDtypeStruct(measured.shape, f32)),
         cost_estimate=cost(1 << 24),
         compiler_params=LIMIT, name="unpack",
     )(on_chip(arrived))
-    entries = angles * rows * depth * groups * lax.axis_size("gz")
-    misfit = square / entries
     return gradient, resid, misfit
 
 

time: 82.2 us -> 81.5 us (level)
  waiting for transfers between devices: 7.57 us -> 6.14 us
  starting transfers between devices: 34.1 us -> 35.5 us
    ppermute x1, waiting for transfers between devices: 1.94 us -> 0.51 us  [butterfly(): x = x + lax.ppermute(x, axis, [(i, i ^ step) for i in range(count)])]
    ppermute x1, starting transfers between devices: 0.64 us -> 2 us  [butterfly(): x = x + lax.ppermute(x, axis, [(i, i ^ step) for i in range(count)])]
where the time goes in v7:
time: 81.5 us; the launch traced here: 81.2 us
  starting transfers between devices  35.5 us (44%)
  blocking collectives  26.5 us (33%)
  Pallas kernels  9.32 us (11%)
  waiting for transfers between devices  6.14 us (8%)
  between operations  3.1 us (4%)
    all_to_all x1, blocking collectives, body(): arrived = lax.all_to_all(payload, ('gx', 'gy'), 0, 0, tiled=True)  26.5 us
    ppermute x3, starting transfers between devices, body(): part = jnp.stack([part, lax.ppermute(part, axis, pairs)])  25.4 us
    all_to_all x1, starting transfers between devices, body(): arrived = lax.all_to_all(payload, ('gx', 'gy'), 0, 0, tiled=True)  7.41 us
    ppermute x3, waiting for transfers between devices, body(): part = jnp.stack([part, lax.ppermute(part, axis, pairs)])  5.63 us
    pallas_call x1, Pallas kernels, body(): pl.pallas_call(functools.partial(main_kernel, dims), out_shape=pltpu.VMEM...  5.53 us
    pallas_call x1, Pallas kernels, body(): pl.pallas_call(pack_kernel, out_shape=(pltpu.VMEM((peers, moved, LANES),...  2.31 us
    ppermute x1, starting transfers between devices, butterfly(): x = x + lax.ppermute(x, axis, [(i, i ^ step) for i in range(count)])  2 us
  transfers between devices with their start and end apart: 6, of which 4 were waited for; matrix products, arithmetic and copies ran while one was open for 0% of the time, Pallas kernels for 2%

profile of v7, /device:TPU:0, one launch (start us, length us, event | category | flops | bytes accessed | tf_op | source)
XLA Modules:
  0.0 81.2 jit_solution(5223147077816992309)
XLA Ops:
  0.6 2.3 %pack.1 = (f32[16,96,128]{2,1,0:T(8,128)}, f32[72,128]{1,0:T(8,128)S(1)}) custom-call(f32[16,64,128]{2,1,0:T(8,128)} %vol_ref.1, f32[8,64,128]{2,1,0:T(8,128)} %meas_ref.1, f32[128,64]{1,0:T(8,128)} %bitcast.14, s32[1,64]{1,0:T(1,128)} %bitcast.17), custom_call_target="tpu_custom_call" | custom-call | tf_op jit(solution)/shard_map/pack/pallas_call | solution.py:340
  2.9 7.4 %all-to-all-start = ((f32[16,96,128]{2,1,0:T(8,128)}), f32[16,96,128]{2,1,0:T(8,128)S(1)}, u32[]{:S(2)}, u32[]{:S(2)}) async-start(f32[16,96,128]{2,1,0:T(8,128)} %get-tuple-element.10), calls=%async_computation | async-start | bytes 1572864 | tf_op jit(solution)/shard_map/all_to_all | solution.py:352
  10.4 0.7 collective-permute-start
  11.0 0.0 collective-permute-done
  11.0 15.3 %collective-permute-start.1 = (f32[72,128]{1,0:T(8,128)S(1)}, f32[72,128]{1,0:T(8,128)S(1)}, u32[]{:S(2)}, u32[]{:S(2)}) collective-permute-start(f32[72,128]{1,0:T(8,128)S(1)} %collective-permute-done), channel_id=1, source_target_pairs={{0,1},{1,0},{2,3},{3,2},{4,5},{5,4},{6,7},{7,6},{8,9},{9,8},{10,11... | collective-permute-start | bytes 110600 | tf_op jit(solution)/shard_map/ppermute | solution.py:355
  26.4 1.9 %collective-permute-done.1 = f32[72,128]{1,0:T(8,128)S(1)} collective-permute-done((f32[72,128]{1,0:T(8,128)S(1)}, f32[72,128]{1,0:T(8,128)S(1)}, u32[]{:S(2)}, u32[]{:S(2)}) %collective-permute-start.1) | collective-permute-done | bytes 36896 | tf_op jit(solution)/shard_map/ppermute | solution.py:355
  28.3 10.0 %collective-permute-start.2 = (f32[2,72,128]{2,1,0:T(8,128)S(1)}, f32[2,72,128]{2,1,0:T(8,128)S(1)}, u32[]{:S(2)}, u32[]{:S(2)}) collective-permute-start(f32[2,72,128]{2,1,0:T(8,128)S(1)} %get-tuple-element.20), channel_id=1, source_target_pairs={{0,2},{2,0},{1,3},{3,1},{4,6},{6,4},{5,7},{7,5},{8,10},{10,8},{9,1... | collective-permute-start | bytes 221192 | tf_op jit(solution)/shard_map/ppermute | solution.py:355
  38.3 2.3 %collective-permute-done.2 = f32[2,72,128]{2,1,0:T(8,128)S(1)} collective-permute-done((f32[2,72,128]{2,1,0:T(8,128)S(1)}, f32[2,72,128]{2,1,0:T(8,128)S(1)}, u32[]{:S(2)}, u32[]{:S(2)}) %collective-permute-start.2) | collective-permute-done | bytes 73760 | tf_op jit(solution)/shard_map/ppermute | solution.py:355
  40.7 0.1 collective-permute-start.3
  40.8 1.4 %collective-permute-done.3 = f32[2,2,72,128]{3,2,1,0:T(8,128)S(1)} collective-permute-done((f32[2,2,72,128]{3,2,1,0:T(8,128)S(1)}, f32[2,2,72,128]{3,2,1,0:T(8,128)S(1)}, u32[]{:S(2)}, u32[]{:S(2)}) %collective-permute-start.3) | collective-permute-done | bytes 147488 | tf_op jit(solution)/shard_map/ppermute | solution.py:355
  42.2 0.4 prepare.1
  42.6 0.0 all-to-all-done.in_ref
  42.6 5.5 %both_ways.1 = f32[16,104,128]{2,1,0:T(8,128)S(1)} custom-call(f32[16,96,128]{2,1,0:T(8,128)S(1)} %all-to-all-done.in_ref, bf16[8,128,256]{2,1,0:T(8,128)(2,1)S(1)} %get-tuple-element.12.wf_ref, bf16[8,128,192]{2,1,0:T(8,128)(2,1)S(1)} %get-tuple-element.13.wb_ref, s32[16,128]{1,0:T(8,128)S(1)} %get-tuple-element.14.int_ref), custom_call_target="tpu_custom_call" | custom-call | tf_op jit(solution)/shard_map/both_ways/pallas_call | solution.py:367
  48.1 26.5 %all_to_all.10.in_ref = f32[16,104,128]{2,1,0:T(8,128)S(1)} all-to-all(f32[16,104,128]{2,1,0:T(8,128)S(1)} %both_ways.1), channel_id=1, replica_groups=mesh['gx'=8,'gy'=2,'gz'=2] {'gx','gy'}, dimensions={0} | all-to-all | bytes 1703936 | tf_op jit(solution)/shard_map/all_to_all | solution.py:373
  74.6 0.6 slice_reduce_fusion
  75.8 2.0 %collective-permute-start.4 = (f32[]{:T(128)}, f32[]{:T(128)}, u32[]{:S(2)}, u32[]{:S(2)}) collective-permute-start(f32[]{:T(128)} %div.3), channel_id=1, source_target_pairs={{0,1},{1,0},{2,3},{3,2},{4,5},{5,4},{6,7},{7,6},{8,9},{9,8},{10,11... | collective-permute-start | bytes 20 | tf_op jit(solution)/shard_map/ppermute | solution.py:237
  77.8 1.1 %unpack.1 = (f32[16,64,128]{2,1,0:T(8,128)}, f32[8,64,128]{2,1,0:T(8,128)}) custom-call(f32[16,104,128]{2,1,0:T(8,128)S(1)} %all_to_all.10.in_ref), custom_call_target="tpu_custom_call" | custom-call | flops 16777216 | bytes 2097152 | tf_op jit(solution)/shard_map/unpack/pallas_call | solution.py:376
  78.9 0.5 collective-permute-done.4
  (3 shorter events, 0.1 us)
Async XLA Ops:
  2.9 39.6 %all-to-all-start = ((f32[16,96,128]{2,1,0:T(8,128)}), f32[16,96,128]{2,1,0:T(8,128)S(1)}, u32[]{:S(2)}, u32[]{:S(2)}) async-start(f32[16,96,128]{2,1,0:T(8,128)} %get-tuple-element.10), calls=%async_computation | async-start | bytes 1572864 | tf_op jit(solution)/shard_map/all_to_all | solution.py:352
  10.4 0.7 collective-permute-start
  11.0 17.3 %collective-permute-start.1 = (f32[72,128]{1,0:T(8,128)S(1)}, f32[72,128]{1,0:T(8,128)S(1)}, u32[]{:S(2)}, u32[]{:S(2)}) collective-permute-start(f32[72,128]{1,0:T(8,128)S(1)} %collective-permute-done), channel_id=1, source_target_pairs={{0,1},{1,0},{2,3},{3,2},{4,5},{5,4},{6,7},{7,6},{8,9},{9,8},{10,11... | collective-permute-start | bytes 110600 | tf_op jit(solution)/shard_map/ppermute | solution.py:355
  28.3 12.3 %collective-permute-start.2 = (f32[2,72,128]{2,1,0:T(8,128)S(1)}, f32[2,72,128]{2,1,0:T(8,128)S(1)}, u32[]{:S(2)}, u32[]{:S(2)}) collective-permute-start(f32[2,72,128]{2,1,0:T(8,128)S(1)} %get-tuple-element.20), channel_id=1, source_target_pairs={{0,2},{2,0},{1,3},{3,1},{4,6},{6,4},{5,7},{7,5},{8,10},{10,8},{9,1... | collective-permute-start | bytes 221192 | tf_op jit(solution)/shard_map/ppermute | solution.py:355
  40.7 1.4 %collective-permute-start.3 = (f32[2,2,72,128]{3,2,1,0:T(8,128)S(1)}, f32[2,2,72,128]{3,2,1,0:T(8,128)S(1)}, u32[]{:S(2)}, u32[]{:S(2)}) collective-permute-start(f32[2,2,72,128]{3,2,1,0:T(8,128)S(1)} %get-tuple-element.18), channel_id=1, source_target_pairs={{0,4},{4,0},{8,12},{12,8},{16,20},{20,16},{24,28},{28,24},{1,5},{5... | collective-permute-start | bytes 442376 | tf_op jit(solution)/shard_map/ppermute | solution.py:355
  75.8 3.6 %collective-permute-start.4 = (f32[]{:T(128)}, f32[]{:T(128)}, u32[]{:S(2)}, u32[]{:S(2)}) collective-permute-start(f32[]{:T(128)} %div.3), channel_id=1, source_target_pairs={{0,1},{1,0},{2,3},{3,2},{4,5},{5,4},{6,7},{7,6},{8,9},{9,8},{10,11... | collective-permute-start | bytes 20 | tf_op jit(solution)/shard_map/ppermute | solution.py:237

commit v8 on v7

--- a/solution.py
+++ b/solution.py
@@ -196,19 +196,26 @@
     ]
 
 
-def unpack_kernel(in_ref, grad_ref, res_ref):
+def unpack(in_ref, at, out_ref):
     peers = in_ref.shape[0]
-    cols, rows, depth = grad_ref.shape
-    share = res_ref.shape[0]
+    count, rows, depth = out_ref.shape
     deep = depth // peers
     second = lax.axis_index("gy")
-    at = 0
-    for ref, count in ((grad_ref, cols // 2), (res_ref, share // 2)):
-        for j in range(count):
-            both = in_ref[:, at : at + deep, :].reshape(depth, LANES).T
-            ref[j + second * count] = both[:rows]
-            ref[j + (1 - second) * count] = both[rows:]
-            at += deep
+    for j in range(count // 2):
+        both = in_ref[:, at : at + deep, :].reshape(depth, LANES).T
+        out_ref[j + second * (count // 2)] = both[:rows]
+        out_ref[j + (1 - second) * (count // 2)] = both[rows:]
+        at += deep
+
+
+def gradient_kernel(in_ref, grad_ref):
+    unpack(in_ref, 0, grad_ref)
+
+
+def residual_kernel(entries, in_ref, own_ref, other_ref, res_ref, misfit_ref):
+    cut = in_ref.shape[1] - SUBS
+    unpack(in_ref, cut - res_ref.shape[0] // 2 * (res_ref.shape[2] // in_ref.shape[0]), res_ref)
+    misfit_ref[...] = jnp.sum(own_ref[...] + other_ref[...], keepdims=True) / entries
 
 
 def cost(flops):
@@ -228,15 +235,6 @@
     planes = sizes[1] * sizes[2]
     pairs = [(at * planes + q, (at ^ (2 * q)) * planes + q) for at in range(sizes[0]) for q in range(planes)]
     return lax.ppermute(x, ("gx", "gy", "gz"), pairs)
-
-
-def butterfly(x, axis):
-    count = lax.axis_size(axis)
-    step = 1
-    while step < count:
-        x = x + lax.ppermute(x, axis, [(i, i ^ step) for i in range(count)])
-        step *= 2
-    return x
 
 
 def passed_along(x, axis, by):
@@ -372,13 +370,22 @@
     )(on_chip(arrived), *map(on_chip, prepared))
     arrived = lax.all_to_all(payload, ("gx", "gy"), 0, 0, tiled=True)
     entries = angles * rows * depth * groups * lax.axis_size("gz")
-    misfit = butterfly(jnp.sum(arrived[:, moved:]) / entries, "gz")
-    gradient, resid = pl.pallas_call(
-        unpack_kernel,
-        out_shape=(jax.ShapeDtypeStruct(volume.shape, f32), jax.ShapeDtypeStruct(measured.shape, f32)),
+    own = jnp.sum(arrived[:, moved:], axis=0)
+    other = lax.ppermute(own, "gz", [(0, 1), (1, 0)])
+    gradient = pl.pallas_call(
+        gradient_kernel,
+        out_shape=jax.ShapeDtypeStruct(volume.shape, f32),
         cost_estimate=cost(1 << 24),
-        compiler_params=LIMIT, name="unpack",
+        compiler_params=LIMIT,
+        name="gradient",
     )(on_chip(arrived))
+    resid, misfit = pl.pallas_call(
+        functools.partial(residual_kernel, entries),
+        out_shape=(jax.ShapeDtypeStruct(measured.shape, f32), jax.ShapeDtypeStruct((1, 1), f32)),
+        compiler_params=LIMIT,
+        name="residual",
+    )(on_chip(arrived), on_chip(own), on_chip(other))
+    misfit = misfit.reshape(())
     return gradient, resid, misfit
 
 

time: 81.5 us -> 79.4 us (0.974)
  between operations: 3.1 us -> 0.69 us
  waiting for transfers between devices: 6.14 us -> 7.6 us
  starting transfers between devices: 35.5 us -> 34.2 us
    ppermute x1, waiting for transfers between devices: 0.51 us -> 1.97 us  [body(): other = lax.ppermute(own, 'gz', [(0, 1), (1, 0)])]
    ppermute x1, starting transfers between devices: 2 us -> 0.7 us  [body(): other = lax.ppermute(own, 'gz', [(0, 1), (1, 0)])]
    pallas_call x1 -> x2, Pallas kernels: 1.08 us -> 1.87 us  [the longest x1 0.99 us: body(): pl.pallas_call(gradient_kernel, out_shape=jax.ShapeDtypeStruct(volume.sha...]
where the time goes in v8:
time: 79.4 us; the launch traced here: 79.1 us
  starting transfers between devices  34.2 us (43%)
  blocking collectives  26.5 us (33%)
  Pallas kernels  10.1 us (13%)
  waiting for transfers between devices  7.6 us (10%)
    all_to_all x1, blocking collectives, body(): arrived = lax.all_to_all(payload, ('gx', 'gy'), 0, 0, tiled=True)  26.5 us
    ppermute x3, starting transfers between devices, body(): part = jnp.stack([part, lax.ppermute(part, axis, pairs)])  25.4 us
    all_to_all x1, starting transfers between devices, body(): arrived = lax.all_to_all(payload, ('gx', 'gy'), 0, 0, tiled=True)  7.41 us
    ppermute x3, waiting for transfers between devices, body(): part = jnp.stack([part, lax.ppermute(part, axis, pairs)])  5.63 us
    pallas_call x1, Pallas kernels, body(): pl.pallas_call(functools.partial(main_kernel, dims), out_shape=pltpu.VMEM...  5.53 us
    pallas_call x1, Pallas kernels, body(): pl.pallas_call(pack_kernel, out_shape=(pltpu.VMEM((peers, moved, LANES),...  2.31 us
    ppermute x1, waiting for transfers between devices, body(): other = lax.ppermute(own, 'gz', [(0, 1), (1, 0)])  1.97 us
  transfers between devices with their start and end apart: 6, of which 4 were waited for; matrix products, arithmetic and copies ran while one was open for 0% of the time, Pallas kernels for 2%

profile of v8, /device:TPU:0, one launch (start us, length us, event | category | flops | bytes accessed | tf_op | source)
XLA Modules:
  0.0 79.1 jit_solution(4068635658812569677)
XLA Ops:
  0.6 2.3 %pack.1 = (f32[16,96,128]{2,1,0:T(8,128)}, f32[72,128]{1,0:T(8,128)S(1)}) custom-call(f32[16,64,128]{2,1,0:T(8,128)} %vol_ref.1, f32[8,64,128]{2,1,0:T(8,128)} %meas_ref.1, f32[128,64]{1,0:T(8,128)} %bitcast.15, s32[1,64]{1,0:T(1,128)} %bitcast.18), custom_call_target="tpu_custom_call" | custom-call | tf_op jit(solution)/shard_map/pack/pallas_call | solution.py:338
  2.9 7.4 %all-to-all-start = ((f32[16,96,128]{2,1,0:T(8,128)}), f32[16,96,128]{2,1,0:T(8,128)S(1)}, u32[]{:S(2)}, u32[]{:S(2)}) async-start(f32[16,96,128]{2,1,0:T(8,128)} %get-tuple-element.10), calls=%async_computation | async-start | bytes 1572864 | tf_op jit(solution)/shard_map/all_to_all | solution.py:350
  10.4 0.7 collective-permute-start
  11.0 0.0 collective-permute-done
  11.0 15.3 %collective-permute-start.1 = (f32[72,128]{1,0:T(8,128)S(1)}, f32[72,128]{1,0:T(8,128)S(1)}, u32[]{:S(2)}, u32[]{:S(2)}) collective-permute-start(f32[72,128]{1,0:T(8,128)S(1)} %collective-permute-done), channel_id=1, source_target_pairs={{0,1},{1,0},{2,3},{3,2},{4,5},{5,4},{6,7},{7,6},{8,9},{9,8},{10,11... | collective-permute-start | bytes 110600 | tf_op jit(solution)/shard_map/ppermute | solution.py:353
  26.4 1.9 %collective-permute-done.1 = f32[72,128]{1,0:T(8,128)S(1)} collective-permute-done((f32[72,128]{1,0:T(8,128)S(1)}, f32[72,128]{1,0:T(8,128)S(1)}, u32[]{:S(2)}, u32[]{:S(2)}) %collective-permute-start.1) | collective-permute-done | bytes 36896 | tf_op jit(solution)/shard_map/ppermute | solution.py:353
  28.3 10.0 %collective-permute-start.2 = (f32[2,72,128]{2,1,0:T(8,128)S(1)}, f32[2,72,128]{2,1,0:T(8,128)S(1)}, u32[]{:S(2)}, u32[]{:S(2)}) collective-permute-start(f32[2,72,128]{2,1,0:T(8,128)S(1)} %get-tuple-element.20), channel_id=1, source_target_pairs={{0,2},{2,0},{1,3},{3,1},{4,6},{6,4},{5,7},{7,5},{8,10},{10,8},{9,1... | collective-permute-start | bytes 221192 | tf_op jit(solution)/shard_map/ppermute | solution.py:353
  38.3 2.3 %collective-permute-done.2 = f32[2,72,128]{2,1,0:T(8,128)S(1)} collective-permute-done((f32[2,72,128]{2,1,0:T(8,128)S(1)}, f32[2,72,128]{2,1,0:T(8,128)S(1)}, u32[]{:S(2)}, u32[]{:S(2)}) %collective-permute-start.2) | collective-permute-done | bytes 73760 | tf_op jit(solution)/shard_map/ppermute | solution.py:353
  40.7 0.1 collective-permute-start.3
  40.8 1.4 %collective-permute-done.3 = f32[2,2,72,128]{3,2,1,0:T(8,128)S(1)} collective-permute-done((f32[2,2,72,128]{3,2,1,0:T(8,128)S(1)}, f32[2,2,72,128]{3,2,1,0:T(8,128)S(1)}, u32[]{:S(2)}, u32[]{:S(2)}) %collective-permute-start.3) | collective-permute-done | bytes 147488 | tf_op jit(solution)/shard_map/ppermute | solution.py:353
  42.2 0.4 prepare.1
  42.6 0.0 all-to-all-done.in_ref
  42.6 5.5 %both_ways.1 = f32[16,104,128]{2,1,0:T(8,128)S(1)} custom-call(f32[16,96,128]{2,1,0:T(8,128)S(1)} %all-to-all-done.in_ref, bf16[8,128,256]{2,1,0:T(8,128)(2,1)S(1)} %get-tuple-element.12.wf_ref, bf16[8,128,192]{2,1,0:T(8,128)(2,1)S(1)} %get-tuple-element.13.wb_ref, s32[16,128]{1,0:T(8,128)S(1)} %get-tuple-element.14.int_ref), custom_call_target="tpu_custom_call" | custom-call | tf_op jit(solution)/shard_map/both_ways/pallas_call | solution.py:365
  48.1 26.5 %all_to_all.10.in_ref = f32[16,104,128]{2,1,0:T(8,128)S(1)} all-to-all(f32[16,104,128]{2,1,0:T(8,128)S(1)} %both_ways.1), channel_id=1, replica_groups=mesh['gx'=8,'gy'=2,'gz'=2] {'gx','gy'}, dimensions={0} | all-to-all | bytes 1703936 | tf_op jit(solution)/shard_map/all_to_all | solution.py:371
  74.6 0.7 collective-permute-start.4
  75.3 1.0 %gradient.1 = f32[16,64,128]{2,1,0:T(8,128)} custom-call(f32[16,104,128]{2,1,0:T(8,128)S(1)} %all_to_all.10.in_ref), custom_call_target="tpu_custom_call" | custom-call | flops 16777216 | bytes 2097152 | tf_op jit(solution)/shard_map/gradient/pallas_call | solution.py:375
  76.3 2.0 %collective-permute-done.4.other_ref = f32[8,128]{1,0:T(8,128)S(1)} collective-permute-done((f32[8,128]{1,0:T(8,128)S(1)}, f32[8,128]{1,0:T(8,128)S(1)}, u32[]{:S(2)}, u32[]{:S(2)}) %collective-permute-start.4) | collective-permute-done | bytes 4128 | tf_op jit(solution)/shard_map/ppermute | solution.py:374
  78.3 0.9 %residual.1 = (f32[8,64,128]{2,1,0:T(8,128)}, f32[1,1]{1,0:T(1,128)}) custom-call(f32[16,104,128]{2,1,0:T(8,128)S(1)} %all_to_all.10.in_ref, f32[8,128]{1,0:T(8,128)S(1)} %slice_reduce_fusion.own_ref, f32[8,128]{1,0:T(8,128)S(1)} %collective-permute-done.4.other_ref), custom_call_target="tpu_custom_call" | custom-call | tf_op jit(solution)/shard_map/residual/pallas_call | solution.py:382
  (4 shorter events, 0.1 us)
Async XLA Ops:
  2.9 39.6 %all-to-all-start = ((f32[16,96,128]{2,1,0:T(8,128)}), f32[16,96,128]{2,1,0:T(8,128)S(1)}, u32[]{:S(2)}, u32[]{:S(2)}) async-start(f32[16,96,128]{2,1,0:T(8,128)} %get-tuple-element.10), calls=%async_computation | async-start | bytes 1572864 | tf_op jit(solution)/shard_map/all_to_all | solution.py:350
  10.4 0.7 collective-permute-start
  11.0 17.3 %collective-permute-start.1 = (f32[72,128]{1,0:T(8,128)S(1)}, f32[72,128]{1,0:T(8,128)S(1)}, u32[]{:S(2)}, u32[]{:S(2)}) collective-permute-start(f32[72,128]{1,0:T(8,128)S(1)} %collective-permute-done), channel_id=1, source_target_pairs={{0,1},{1,0},{2,3},{3,2},{4,5},{5,4},{6,7},{7,6},{8,9},{9,8},{10,11... | collective-permute-start | bytes 110600 | tf_op jit(solution)/shard_map/ppermute | solution.py:353
  28.3 12.3 %collective-permute-start.2 = (f32[2,72,128]{2,1,0:T(8,128)S(1)}, f32[2,72,128]{2,1,0:T(8,128)S(1)}, u32[]{:S(2)}, u32[]{:S(2)}) collective-permute-start(f32[2,72,128]{2,1,0:T(8,128)S(1)} %get-tuple-element.20), channel_id=1, source_target_pairs={{0,2},{2,0},{1,3},{3,1},{4,6},{6,4},{5,7},{7,5},{8,10},{10,8},{9,1... | collective-permute-start | bytes 221192 | tf_op jit(solution)/shard_map/ppermute | solution.py:353
  40.7 1.4 %collective-permute-start.3 = (f32[2,2,72,128]{3,2,1,0:T(8,128)S(1)}, f32[2,2,72,128]{3,2,1,0:T(8,128)S(1)}, u32[]{:S(2)}, u32[]{:S(2)}) collective-permute-start(f32[2,2,72,128]{3,2,1,0:T(8,128)S(1)} %get-tuple-element.18), channel_id=1, source_target_pairs={{0,4},{4,0},{8,12},{12,8},{16,20},{20,16},{24,28},{28,24},{1,5},{5... | collective-permute-start | bytes 442376 | tf_op jit(solution)/shard_map/ppermute | solution.py:353
  74.6 3.7 %collective-permute-start.4 = (f32[8,128]{1,0:T(8,128)S(1)}, f32[8,128]{1,0:T(8,128)S(1)}, u32[]{:S(2)}, u32[]{:S(2)}) collective-permute-start(f32[8,128]{1,0:T(8,128)S(1)} %slice_reduce_fusion.own_ref), channel_id=1, source_target_pairs={{0,1},{1,0},{2,3},{3,2},{4,5},{5,4},{6,7},{7,6},{8,9},{9,8},{10,11... | collective-permute-start | bytes 12296 | tf_op jit(solution)/shard_map/ppermute | solution.py:374

commit v9 on v8

--- a/solution.py
+++ b/solution.py
@@ -208,14 +208,13 @@
         at += deep
 
 
-def gradient_kernel(in_ref, grad_ref):
+def unpack_kernel(in_ref, grad_ref, res_ref):
     unpack(in_ref, 0, grad_ref)
-
-
-def residual_kernel(entries, in_ref, own_ref, other_ref, res_ref, misfit_ref):
-    cut = in_ref.shape[1] - SUBS
-    unpack(in_ref, cut - res_ref.shape[0] // 2 * (res_ref.shape[2] // in_ref.shape[0]), res_ref)
-    misfit_ref[...] = jnp.sum(own_ref[...] + other_ref[...], keepdims=True) / entries
+    unpack(in_ref, grad_ref.shape[0] // 2 * (grad_ref.shape[2] // in_ref.shape[0]), res_ref)
+
+
+def misfit_kernel(entries, own_ref, other_ref, out_ref):
+    out_ref[...] = jnp.sum(own_ref[...] + other_ref[...], keepdims=True) / entries
 
 
 def cost(flops):
@@ -310,7 +309,7 @@
     return (
         groups == 2
         and lax.axis_size("gz") == 2
-        and lax.axis_size("gx") == 8
+        and lax.axis_size("gx") == 2 * groups * lax.axis_size("gz")
         and 2 * rows == LANES
         and depth == LANES
         and rest == 0
@@ -372,19 +371,19 @@
     entries = angles * rows * depth * groups * lax.axis_size("gz")
     own = jnp.sum(arrived[:, moved:], axis=0)
     other = lax.ppermute(own, "gz", [(0, 1), (1, 0)])
-    gradient = pl.pallas_call(
-        gradient_kernel,
-        out_shape=jax.ShapeDtypeStruct(volume.shape, f32),
+    gradient, resid = pl.pallas_call(
+        unpack_kernel,
+        out_shape=(jax.ShapeDtypeStruct(volume.shape, f32), jax.ShapeDtypeStruct(measured.shape, f32)),
         cost_estimate=cost(1 << 24),
         compiler_params=LIMIT,
-        name="gradient",
+        name="unpack",
     )(on_chip(arrived))
-    resid, misfit = pl.pallas_call(
-        functools.partial(residual_kernel, entries),
-        out_shape=(jax.ShapeDtypeStruct(measured.shape, f32), jax.ShapeDtypeStruct((1, 1), f32)),
+    misfit = pl.pallas_call(
+        functools.partial(misfit_kernel, entries),
+        out_shape=jax.ShapeDtypeStruct((1, 1), f32),
         compiler_params=LIMIT,
-        name="residual",
-    )(on_chip(arrived), on_chip(own), on_chip(other))
+        name="misfit",
+    )(on_chip(own), on_chip(other))
     misfit = misfit.reshape(())
     return gradient, resid, misfit
 

time: 79.4 us -> 79.2 us (level)
  no operation moved by 1% of the time
where the time goes in v9:
time: 79.2 us; the launch traced here: 78.9 us
  starting transfers between devices  34.2 us (43%)
  blocking collectives  26.5 us (33%)
  Pallas kernels  9.95 us (13%)
  waiting for transfers between devices  7.52 us (9%)
    all_to_all x1, blocking collectives, body(): arrived = lax.all_to_all(payload, ('gx', 'gy'), 0, 0, tiled=True)  26.5 us
    ppermute x3, starting transfers between devices, body(): part = jnp.stack([part, lax.ppermute(part, axis, pairs)])  25.4 us
    all_to_all x1, starting transfers between devices, body(): arrived = lax.all_to_all(payload, ('gx', 'gy'), 0, 0, tiled=True)  7.41 us
    ppermute x3, waiting for transfers between devices, body(): part = jnp.stack([part, lax.ppermute(part, axis, pairs)])  5.63 us
    pallas_call x1, Pallas kernels, body(): pl.pallas_call(functools.partial(main_kernel, dims), out_shape=pltpu.VMEM...  5.53 us
    pallas_call x1, Pallas kernels, body(): pl.pallas_call(pack_kernel, out_shape=(pltpu.VMEM((peers, moved, LANES),...  2.31 us
    ppermute x1, waiting for transfers between devices, body(): other = lax.ppermute(own, 'gz', [(0, 1), (1, 0)])  1.89 us
  transfers between devices with their start and end apart: 6, of which 4 were waited for; matrix products, arithmetic and copies ran while one was open for 0% of the time, Pallas kernels for 2%

profile of v9, /device:TPU:0, one launch (start us, length us, event | category | flops | bytes accessed | tf_op | source)
XLA Modules:
  0.0 78.9 jit_solution(1722897767686429253)
XLA Ops:
  0.6 2.3 %pack.1 = (f32[16,96,128]{2,1,0:T(8,128)}, f32[72,128]{1,0:T(8,128)S(1)}) custom-call(f32[16,64,128]{2,1,0:T(8,128)} %vol_ref.1, f32[8,64,128]{2,1,0:T(8,128)} %meas_ref.1, f32[128,64]{1,0:T(8,128)} %bitcast.15, s32[1,64]{1,0:T(1,128)} %bitcast.18), custom_call_target="tpu_custom_call" | custom-call | tf_op jit(solution)/shard_map/pack/pallas_call | solution.py:337
  2.9 7.4 %all-to-all-start = ((f32[16,96,128]{2,1,0:T(8,128)}), f32[16,96,128]{2,1,0:T(8,128)S(1)}, u32[]{:S(2)}, u32[]{:S(2)}) async-start(f32[16,96,128]{2,1,0:T(8,128)} %get-tuple-element.10), calls=%async_computation | async-start | bytes 1572864 | tf_op jit(solution)/shard_map/all_to_all | solution.py:349
  10.4 0.7 collective-permute-start
  11.0 0.0 collective-permute-done
  11.0 15.3 %collective-permute-start.1 = (f32[72,128]{1,0:T(8,128)S(1)}, f32[72,128]{1,0:T(8,128)S(1)}, u32[]{:S(2)}, u32[]{:S(2)}) collective-permute-start(f32[72,128]{1,0:T(8,128)S(1)} %collective-permute-done), channel_id=1, source_target_pairs={{0,1},{1,0},{2,3},{3,2},{4,5},{5,4},{6,7},{7,6},{8,9},{9,8},{10,11... | collective-permute-start | bytes 110600 | tf_op jit(solution)/shard_map/ppermute | solution.py:352
  26.4 1.9 %collective-permute-done.1 = f32[72,128]{1,0:T(8,128)S(1)} collective-permute-done((f32[72,128]{1,0:T(8,128)S(1)}, f32[72,128]{1,0:T(8,128)S(1)}, u32[]{:S(2)}, u32[]{:S(2)}) %collective-permute-start.1) | collective-permute-done | bytes 36896 | tf_op jit(solution)/shard_map/ppermute | solution.py:352
  28.3 10.0 %collective-permute-start.2 = (f32[2,72,128]{2,1,0:T(8,128)S(1)}, f32[2,72,128]{2,1,0:T(8,128)S(1)}, u32[]{:S(2)}, u32[]{:S(2)}) collective-permute-start(f32[2,72,128]{2,1,0:T(8,128)S(1)} %get-tuple-element.20), channel_id=1, source_target_pairs={{0,2},{2,0},{1,3},{3,1},{4,6},{6,4},{5,7},{7,5},{8,10},{10,8},{9,1... | collective-permute-start | bytes 221192 | tf_op jit(solution)/shard_map/ppermute | solution.py:352
  38.3 2.3 %collective-permute-done.2 = f32[2,72,128]{2,1,0:T(8,128)S(1)} collective-permute-done((f32[2,72,128]{2,1,0:T(8,128)S(1)}, f32[2,72,128]{2,1,0:T(8,128)S(1)}, u32[]{:S(2)}, u32[]{:S(2)}) %collective-permute-start.2) | collective-permute-done | bytes 73760 | tf_op jit(solution)/shard_map/ppermute | solution.py:352
  40.7 0.1 collective-permute-start.3
  40.8 1.4 %collective-permute-done.3 = f32[2,2,72,128]{3,2,1,0:T(8,128)S(1)} collective-permute-done((f32[2,2,72,128]{3,2,1,0:T(8,128)S(1)}, f32[2,2,72,128]{3,2,1,0:T(8,128)S(1)}, u32[]{:S(2)}, u32[]{:S(2)}) %collective-permute-start.3) | collective-permute-done | bytes 147488 | tf_op jit(solution)/shard_map/ppermute | solution.py:352
  42.2 0.4 prepare.1
  42.6 0.0 all-to-all-done.in_ref
  42.6 5.5 %both_ways.1 = f32[16,104,128]{2,1,0:T(8,128)S(1)} custom-call(f32[16,96,128]{2,1,0:T(8,128)S(1)} %all-to-all-done.in_ref, bf16[8,128,256]{2,1,0:T(8,128)(2,1)S(1)} %get-tuple-element.12.wf_ref, bf16[8,128,192]{2,1,0:T(8,128)(2,1)S(1)} %get-tuple-element.13.wb_ref, s32[16,128]{1,0:T(8,128)S(1)} %get-tuple-element.14.int_ref), custom_call_target="tpu_custom_call" | custom-call | tf_op jit(solution)/shard_map/both_ways/pallas_call | solution.py:364
  48.1 26.5 %all_to_all.10.in_ref = f32[16,104,128]{2,1,0:T(8,128)S(1)} all-to-all(f32[16,104,128]{2,1,0:T(8,128)S(1)} %both_ways.1), channel_id=1, replica_groups=mesh['gx'=8,'gy'=2,'gz'=2] {'gx','gy'}, dimensions={0} | all-to-all | bytes 1703936 | tf_op jit(solution)/shard_map/all_to_all | solution.py:370
  74.6 0.7 collective-permute-start.4
  75.3 1.1 %unpack.1 = (f32[16,64,128]{2,1,0:T(8,128)}, f32[8,64,128]{2,1,0:T(8,128)}) custom-call(f32[16,104,128]{2,1,0:T(8,128)S(1)} %all_to_all.10.in_ref), custom_call_target="tpu_custom_call" | custom-call | flops 16777216 | bytes 2097152 | tf_op jit(solution)/shard_map/unpack/pallas_call | solution.py:374
  76.4 1.9 %collective-permute-done.4.other_ref = f32[8,128]{1,0:T(8,128)S(1)} collective-permute-done((f32[8,128]{1,0:T(8,128)S(1)}, f32[8,128]{1,0:T(8,128)S(1)}, u32[]{:S(2)}, u32[]{:S(2)}) %collective-permute-start.4) | collective-permute-done | bytes 4128 | tf_op jit(solution)/shard_map/ppermute | solution.py:373
  78.3 0.6 misfit.1
  (4 shorter events, 0.1 us)
Async XLA Ops:
  2.9 39.6 %all-to-all-start = ((f32[16,96,128]{2,1,0:T(8,128)}), f32[16,96,128]{2,1,0:T(8,128)S(1)}, u32[]{:S(2)}, u32[]{:S(2)}) async-start(f32[16,96,128]{2,1,0:T(8,128)} %get-tuple-element.10), calls=%async_computation | async-start | bytes 1572864 | tf_op jit(solution)/shard_map/all_to_all | solution.py:349
  10.4 0.7 collective-permute-start
  11.0 17.3 %collective-permute-start.1 = (f32[72,128]{1,0:T(8,128)S(1)}, f32[72,128]{1,0:T(8,128)S(1)}, u32[]{:S(2)}, u32[]{:S(2)}) collective-permute-start(f32[72,128]{1,0:T(8,128)S(1)} %collective-permute-done), channel_id=1, source_target_pairs={{0,1},{1,0},{2,3},{3,2},{4,5},{5,4},{6,7},{7,6},{8,9},{9,8},{10,11... | collective-permute-start | bytes 110600 | tf_op jit(solution)/shard_map/ppermute | solution.py:352
  28.3 12.3 %collective-permute-start.2 = (f32[2,72,128]{2,1,0:T(8,128)S(1)}, f32[2,72,128]{2,1,0:T(8,128)S(1)}, u32[]{:S(2)}, u32[]{:S(2)}) collective-permute-start(f32[2,72,128]{2,1,0:T(8,128)S(1)} %get-tuple-element.20), channel_id=1, source_target_pairs={{0,2},{2,0},{1,3},{3,1},{4,6},{6,4},{5,7},{7,5},{8,10},{10,8},{9,1... | collective-permute-start | bytes 221192 | tf_op jit(solution)/shard_map/ppermute | solution.py:352
  40.7 1.4 %collective-permute-start.3 = (f32[2,2,72,128]{3,2,1,0:T(8,128)S(1)}, f32[2,2,72,128]{3,2,1,0:T(8,128)S(1)}, u32[]{:S(2)}, u32[]{:S(2)}) collective-permute-start(f32[2,2,72,128]{3,2,1,0:T(8,128)S(1)} %get-tuple-element.18), channel_id=1, source_target_pairs={{0,4},{4,0},{8,12},{12,8},{16,20},{20,16},{24,28},{28,24},{1,5},{5... | collective-permute-start | bytes 442376 | tf_op jit(solution)/shard_map/ppermute | solution.py:352
  74.6 3.7 %collective-permute-start.4 = (f32[8,128]{1,0:T(8,128)S(1)}, f32[8,128]{1,0:T(8,128)S(1)}, u32[]{:S(2)}, u32[]{:S(2)}) collective-permute-start(f32[8,128]{1,0:T(8,128)S(1)} %slice_reduce_fusion.own_ref), channel_id=1, source_target_pairs={{0,1},{1,0},{2,3},{3,2},{4,5},{5,4},{6,7},{7,6},{8,9},{9,8},{10,11... | collective-permute-start | bytes 12296 | tf_op jit(solution)/shard_map/ppermute | solution.py:373

commit v10 on v9

--- a/solution.py
+++ b/solution.py
@@ -13,6 +13,7 @@
 LIMIT = pltpu.CompilerParams(vmem_limit_bytes=8 << 20)
 STRIDE = 72
 TOGETHER = 4
+BACK = 4
 
 
 def split(x):
@@ -161,13 +162,6 @@
                 for h, block in enumerate(joined(total[:half], total[half:])):
                     out_ref[i * groups + h, pl.ds(z, half, stride=deep), :] = block
 
-    def backward(n, carry):
-        i = 2 * n
-        for k in range(2):
-            scatter_rows(i + k, turn_refs[k])
-            backproject(i + k, turn_refs[k])
-        return carry
-
     lax.fori_loop(0, bricks // TOGETHER, forward, 0)
     square = jnp.zeros((deep, LANES), jnp.float32)
     for i in range(bricks):
@@ -180,9 +174,22 @@
             square = square + low * low + high * high
             for h, block in enumerate(joined(low, high)):
                 out_ref[i * groups + h, at : at + deep, :] = block
-    for p in range(bricks * groups):
-        out_ref[p, w_at : w_at + deep, :] = square
-    lax.fori_loop(0, bricks // 2, backward, 0)
+
+    def backward(n, carry):
+        i = n * BACK
+        for k in range(BACK):
+            scatter_rows(i + k, turn_refs[k])
+
+        @pl.when(n == 0)
+        def _():
+            for p in range(bricks * groups):
+                out_ref[p, w_at : w_at + deep, :] = square
+
+        for k in range(BACK):
+            backproject(i + k, turn_refs[k])
+        return carry
+
+    lax.fori_loop(0, bricks // BACK, backward, 0)
 
 
 def main_scratch(dims):

time: 79.2 us -> 79 us (level)
  no operation moved by 1% of the time
where the time goes in v10:
time: 79 us; the launch traced here: 78.7 us
  starting transfers between devices  34.2 us (43%)
  blocking collectives  26.5 us (34%)
  Pallas kernels  9.75 us (12%)
  waiting for transfers between devices  7.52 us (10%)
    all_to_all x1, blocking collectives, body(): arrived = lax.all_to_all(payload, ('gx', 'gy'), 0, 0, tiled=True)  26.5 us
    ppermute x3, starting transfers between devices, body(): part = jnp.stack([part, lax.ppermute(part, axis, pairs)])  25.4 us
    all_to_all x1, starting transfers between devices, body(): arrived = lax.all_to_all(payload, ('gx', 'gy'), 0, 0, tiled=True)  7.41 us
    ppermute x3, waiting for transfers between devices, body(): part = jnp.stack([part, lax.ppermute(part, axis, pairs)])  5.63 us
    pallas_call x1, Pallas kernels, body(): pl.pallas_call(functools.partial(main_kernel, dims), out_shape=pltpu.VMEM...  5.33 us
    pallas_call x1, Pallas kernels, body(): pl.pallas_call(pack_kernel, out_shape=(pltpu.VMEM((peers, moved, LANES),...  2.31 us
    ppermute x1, waiting for transfers between devices, body(): other = lax.ppermute(own, 'gz', [(0, 1), (1, 0)])  1.89 us
  transfers between devices with their start and end apart: 6, of which 4 were waited for; matrix products, arithmetic and copies ran while one was open for 0% of the time, Pallas kernels for 2%

profile of v10, /device:TPU:0, one launch (start us, length us, event | category | flops | bytes accessed | tf_op | source)
XLA Modules:
  0.0 78.7 jit_solution(6325519602965455659)
XLA Ops:
  0.6 2.3 %pack.1 = (f32[16,96,128]{2,1,0:T(8,128)}, f32[72,128]{1,0:T(8,128)S(1)}) custom-call(f32[16,64,128]{2,1,0:T(8,128)} %vol_ref.1, f32[8,64,128]{2,1,0:T(8,128)} %meas_ref.1, f32[128,64]{1,0:T(8,128)} %bitcast.15, s32[1,64]{1,0:T(1,128)} %bitcast.18), custom_call_target="tpu_custom_call" | custom-call | tf_op jit(solution)/shard_map/pack/pallas_call | solution.py:344
  2.9 7.4 %all-to-all-start = ((f32[16,96,128]{2,1,0:T(8,128)}), f32[16,96,128]{2,1,0:T(8,128)S(1)}, u32[]{:S(2)}, u32[]{:S(2)}) async-start(f32[16,96,128]{2,1,0:T(8,128)} %get-tuple-element.10), calls=%async_computation | async-start | bytes 1572864 | tf_op jit(solution)/shard_map/all_to_all | solution.py:356
  10.4 0.7 collective-permute-start
  11.0 0.0 collective-permute-done
  11.0 15.3 %collective-permute-start.1 = (f32[72,128]{1,0:T(8,128)S(1)}, f32[72,128]{1,0:T(8,128)S(1)}, u32[]{:S(2)}, u32[]{:S(2)}) collective-permute-start(f32[72,128]{1,0:T(8,128)S(1)} %collective-permute-done), channel_id=1, source_target_pairs={{0,1},{1,0},{2,3},{3,2},{4,5},{5,4},{6,7},{7,6},{8,9},{9,8},{10,11... | collective-permute-start | bytes 110600 | tf_op jit(solution)/shard_map/ppermute | solution.py:359
  26.4 1.9 %collective-permute-done.1 = f32[72,128]{1,0:T(8,128)S(1)} collective-permute-done((f32[72,128]{1,0:T(8,128)S(1)}, f32[72,128]{1,0:T(8,128)S(1)}, u32[]{:S(2)}, u32[]{:S(2)}) %collective-permute-start.1) | collective-permute-done | bytes 36896 | tf_op jit(solution)/shard_map/ppermute | solution.py:359
  28.3 10.0 %collective-permute-start.2 = (f32[2,72,128]{2,1,0:T(8,128)S(1)}, f32[2,72,128]{2,1,0:T(8,128)S(1)}, u32[]{:S(2)}, u32[]{:S(2)}) collective-permute-start(f32[2,72,128]{2,1,0:T(8,128)S(1)} %get-tuple-element.20), channel_id=1, source_target_pairs={{0,2},{2,0},{1,3},{3,1},{4,6},{6,4},{5,7},{7,5},{8,10},{10,8},{9,1... | collective-permute-start | bytes 221192 | tf_op jit(solution)/shard_map/ppermute | solution.py:359
  38.3 2.3 %collective-permute-done.2 = f32[2,72,128]{2,1,0:T(8,128)S(1)} collective-permute-done((f32[2,72,128]{2,1,0:T(8,128)S(1)}, f32[2,72,128]{2,1,0:T(8,128)S(1)}, u32[]{:S(2)}, u32[]{:S(2)}) %collective-permute-start.2) | collective-permute-done | bytes 73760 | tf_op jit(solution)/shard_map/ppermute | solution.py:359
  40.7 0.1 collective-permute-start.3
  40.8 1.4 %collective-permute-done.3 = f32[2,2,72,128]{3,2,1,0:T(8,128)S(1)} collective-permute-done((f32[2,2,72,128]{3,2,1,0:T(8,128)S(1)}, f32[2,2,72,128]{3,2,1,0:T(8,128)S(1)}, u32[]{:S(2)}, u32[]{:S(2)}) %collective-permute-start.3) | collective-permute-done | bytes 147488 | tf_op jit(solution)/shard_map/ppermute | solution.py:359
  42.2 0.4 prepare.1
  42.6 0.0 all-to-all-done.in_ref
  42.6 5.3 %both_ways.1 = f32[16,104,128]{2,1,0:T(8,128)S(1)} custom-call(f32[16,96,128]{2,1,0:T(8,128)S(1)} %all-to-all-done.in_ref, bf16[8,128,256]{2,1,0:T(8,128)(2,1)S(1)} %get-tuple-element.12.wf_ref, bf16[8,128,192]{2,1,0:T(8,128)(2,1)S(1)} %get-tuple-element.13.wb_ref, s32[16,128]{1,0:T(8,128)S(1)} %get-tuple-element.14.int_ref), custom_call_target="tpu_custom_call" | custom-call | tf_op jit(solution)/shard_map/both_ways/pallas_call | solution.py:371
  47.9 26.5 %all_to_all.10.in_ref = f32[16,104,128]{2,1,0:T(8,128)S(1)} all-to-all(f32[16,104,128]{2,1,0:T(8,128)S(1)} %both_ways.1), channel_id=1, replica_groups=mesh['gx'=8,'gy'=2,'gz'=2] {'gx','gy'}, dimensions={0} | all-to-all | bytes 1703936 | tf_op jit(solution)/shard_map/all_to_all | solution.py:377
  74.4 0.7 collective-permute-start.4
  75.1 1.1 %unpack.1 = (f32[16,64,128]{2,1,0:T(8,128)}, f32[8,64,128]{2,1,0:T(8,128)}) custom-call(f32[16,104,128]{2,1,0:T(8,128)S(1)} %all_to_all.10.in_ref), custom_call_target="tpu_custom_call" | custom-call | flops 16777216 | bytes 2097152 | tf_op jit(solution)/shard_map/unpack/pallas_call | solution.py:381
  76.2 1.9 %collective-permute-done.4.other_ref = f32[8,128]{1,0:T(8,128)S(1)} collective-permute-done((f32[8,128]{1,0:T(8,128)S(1)}, f32[8,128]{1,0:T(8,128)S(1)}, u32[]{:S(2)}, u32[]{:S(2)}) %collective-permute-start.4) | collective-permute-done | bytes 4128 | tf_op jit(solution)/shard_map/ppermute | solution.py:380
  78.1 0.6 misfit.1
  (4 shorter events, 0.1 us)
Async XLA Ops:
  2.9 39.6 %all-to-all-start = ((f32[16,96,128]{2,1,0:T(8,128)}), f32[16,96,128]{2,1,0:T(8,128)S(1)}, u32[]{:S(2)}, u32[]{:S(2)}) async-start(f32[16,96,128]{2,1,0:T(8,128)} %get-tuple-element.10), calls=%async_computation | async-start | bytes 1572864 | tf_op jit(solution)/shard_map/all_to_all | solution.py:356
  10.4 0.7 collective-permute-start
  11.0 17.3 %collective-permute-start.1 = (f32[72,128]{1,0:T(8,128)S(1)}, f32[72,128]{1,0:T(8,128)S(1)}, u32[]{:S(2)}, u32[]{:S(2)}) collective-permute-start(f32[72,128]{1,0:T(8,128)S(1)} %collective-permute-done), channel_id=1, source_target_pairs={{0,1},{1,0},{2,3},{3,2},{4,5},{5,4},{6,7},{7,6},{8,9},{9,8},{10,11... | collective-permute-start | bytes 110600 | tf_op jit(solution)/shard_map/ppermute | solution.py:359
  28.3 12.3 %collective-permute-start.2 = (f32[2,72,128]{2,1,0:T(8,128)S(1)}, f32[2,72,128]{2,1,0:T(8,128)S(1)}, u32[]{:S(2)}, u32[]{:S(2)}) collective-permute-start(f32[2,72,128]{2,1,0:T(8,128)S(1)} %get-tuple-element.20), channel_id=1, source_target_pairs={{0,2},{2,0},{1,3},{3,1},{4,6},{6,4},{5,7},{7,5},{8,10},{10,8},{9,1... | collective-permute-start | bytes 221192 | tf_op jit(solution)/shard_map/ppermute | solution.py:359
  40.7 1.4 %collective-permute-start.3 = (f32[2,2,72,128]{3,2,1,0:T(8,128)S(1)}, f32[2,2,72,128]{3,2,1,0:T(8,128)S(1)}, u32[]{:S(2)}, u32[]{:S(2)}) collective-permute-start(f32[2,2,72,128]{3,2,1,0:T(8,128)S(1)} %get-tuple-element.18), channel_id=1, source_target_pairs={{0,4},{4,0},{8,12},{12,8},{16,20},{20,16},{24,28},{28,24},{1,5},{5... | collective-permute-start | bytes 442376 | tf_op jit(solution)/shard_map/ppermute | solution.py:359
  74.4 3.7 %collective-permute-start.4 = (f32[8,128]{1,0:T(8,128)S(1)}, f32[8,128]{1,0:T(8,128)S(1)}, u32[]{:S(2)}, u32[]{:S(2)}) collective-permute-start(f32[8,128]{1,0:T(8,128)S(1)} %slice_reduce_fusion.own_ref), channel_id=1, source_target_pairs={{0,1},{1,0},{2,3},{3,2},{4,5},{5,4},{6,7},{7,6},{8,9},{9,8},{10,11... | collective-permute-start | bytes 12296 | tf_op jit(solution)/shard_map/ppermute | solution.py:380
